TPU v7x, 1024 devices: a whole 4x8x16 slice. The times are simulated.
1024 devices in a mesh: section: 16 (over x_lo, y), replica: 64 (over x_hi, z, core).
Axes of the slice: x: 4 (x_hi: 2, x_lo: 2; x = x_hi * 2 + x_lo), y: 8, z: 16, core: 2. Of those that a mesh axis runs over, the one named last changes fastest.
Arguments:
- gradients: bfloat16 [64, 5120, 1024], P('replica', 'section'), may hold values from -2 to 2
- hidden: bfloat16 [64, 256, 5120], P('replica'), may hold values from -40 to 40
- lengths: int32 [64], P('replica'), may hold values from 64 to 256
- query_weight: bfloat16 [5120, 2560], P(None, 'section'), may hold values from -0.078125 to 0.078125
- master: float32 [16, 64, 5, 1024], P(None, 'replica', None, 'section'), may hold values from -0.078125 to 0.078125
- first_moment: float32 [16, 64, 5, 1024], P(None, 'replica', None, 'section'), may hold values from -3 to 3
- second_moment: float32 [16, 64, 5, 1024], P(None, 'replica', None, 'section'), may hold values from 0.1 to 2
Outputs:
- new_master: float32 [16, 64, 5, 1024], P(None, 'replica', None, 'section')
- new_first: float32 [16, 64, 5, 1024], P(None, 'replica', None, 'section')
- new_second: float32 [16, 64, 5, 1024], P(None, 'replica', None, 'section')
- context: float32 [64, 256, 2560], P('replica', 'section')
All inputs are finite; a program needn't handle non-finite values.
Results may differ from a plain program's by a relative error of at most 0.019.
The roundings to bfloat16 on the way count: a program that leaves them out, or rounds other values in their place, can miss the bound.
Values may be sent and summed in bfloat16 or wider, within the bound.
A program may use at most 32 MiB of HBM per device.

v0:
```python
import jax
import jax.numpy as jnp
from jax import lax
from jax.sharding import PartitionSpec as P

HEAD = 128
KV_HEADS = 4
GROUP = 5
QCOLS = 2560
KCOLS = 512
COLS = 1024


BETA_ONE = 0.9
BETA_TWO = 0.95
EPSILON = 1e-08
DECAY = 0.1
RATE = 0.001
CORRECT_ONE = 1.0 - 0.9**50
CORRECT_TWO = 1.0 - 0.95**50


def cut_along(array, dim, size):
    shape = array.shape
    blocks = array.reshape(*shape[:dim], size, shape[dim] // size, *shape[dim + 1 :])
    return jnp.moveaxis(blocks, dim, 0)


def sent_and_summed(array, axis, dim):
    blocks = cut_along(array, dim, lax.axis_size(axis))
    arrived = lax.all_to_all(blocks, axis, split_axis=0, concat_axis=0, tiled=True)
    return arrived.astype(jnp.float32).sum(axis=0)


def laid_out(blocks, dim):
    blocks = jnp.moveaxis(blocks, 0, dim)
    shape = blocks.shape
    return blocks.reshape(*shape[:dim], shape[dim] * shape[dim + 1], *shape[dim + 2 :])


def copy_for_each(array, axis):
    size = lax.axis_size(axis)
    return lax.all_to_all(
        jnp.broadcast_to(array[None], (size, *array.shape)), axis, 0, 0, tiled=True
    )


def gather_directly(array, axis, dim):
    return laid_out(copy_for_each(array, axis), dim)


def rows_first(arrays, axis, dims):
    turned = [jnp.moveaxis(a, dim, 0) for a, dim in zip(arrays, dims)]
    both = jnp.concatenate([t.reshape(len(t), -1) for t in turned], axis=1)
    filled, at, done = (lax.all_gather(both, axis, axis=0, tiled=True), 0, [])
    for t, dim in zip(turned, dims):
        section = filled[:, at : at + t[0].size].reshape(-1, *t.shape[1:])
        done.append(jnp.moveaxis(section, 0, dim))
        at += t[0].size
    return tuple(done)


def by_rank(matrix, rank_count):
    row_count = matrix.shape[0]
    key_part = matrix[:, :KCOLS].reshape(row_count, rank_count, KCOLS // rank_count)
    value_part = matrix[:, KCOLS:].reshape(row_count, rank_count, KCOLS // rank_count)
    return jnp.concatenate([key_part, value_part], axis=2)


def adam_step(gradient, weight, first_moment, second_moment):
    new_first = BETA_ONE * first_moment + (1.0 - BETA_ONE) * gradient
    new_second = BETA_TWO * second_moment + (1.0 - BETA_TWO) * gradient * gradient
    direction = new_first / CORRECT_ONE / (jnp.sqrt(new_second / CORRECT_TWO) + EPSILON)
    new_master = weight - RATE * (direction + DECAY * weight)
    return (new_master, new_first, new_second)


def attend(queries, key_rows, value_rows, positions, length):
    query_count = queries.shape[0]
    seq_len = key_rows.shape[0]
    grouped = queries.reshape(query_count, KV_HEADS, GROUP, HEAD)
    key_heads = key_rows.reshape(seq_len, KV_HEADS, HEAD)
    value_heads = value_rows.reshape(seq_len, KV_HEADS, HEAD)
    scores = jnp.einsum(
        "tkgd,jkd->kgtj", grouped, key_heads, preferred_element_type=jnp.float32
    ) * HEAD ** (-0.5)
    key_pos = jnp.arange(seq_len, dtype=jnp.int32)
    allowed = (key_pos[None, :] <= positions[:, None]) & (key_pos[None, :] < length)
    scores = jnp.where(allowed[None, None], scores, -jnp.inf)
    row_max = jnp.max(scores, axis=-1, keepdims=True)
    expo = jnp.exp(scores - row_max)
    probs = (expo / jnp.sum(expo, axis=-1, keepdims=True)).astype(jnp.bfloat16)
    mixed = jnp.einsum("kgtj,jkd->tkgd", probs, value_heads, preferred_element_type=jnp.float32)
    mixed = mixed.reshape(query_count, QCOLS)
    live_rows = positions < length
    return jnp.where(live_rows[:, None], mixed, 0.0)


def on_device(gradients, hidden, lengths, query_weight, master, first_moment, second_moment):
    rank_count = lax.axis_size("section")
    group_count = lax.axis_size("replica")
    section_index = lax.axis_index("section")
    local_grad = gradients[0].astype(jnp.float32)
    summed = sent_and_summed(local_grad.astype(jnp.bfloat16), "replica", 0)
    slab_rows = summed.shape[0]
    regrouped = by_rank(summed, rank_count).reshape(1, 1, slab_rows, COLS)
    owned_grad = lax.all_to_all(regrouped, "section", split_axis=3, concat_axis=0, tiled=True)
    new_master, new_first, new_second = adam_step(owned_grad, master, first_moment, second_moment)
    weight = new_master.astype(jnp.bfloat16)
    rank_cols = weight.shape[3]
    tokens = hidden[0]
    seq_len = tokens.shape[0]
    piece_rows = rank_count * slab_rows
    spread = (
        tokens.reshape(seq_len, rank_count, group_count, slab_rows)
        .transpose(0, 2, 1, 3)
        .reshape(seq_len, group_count * piece_rows)
    )
    arrived = gather_directly(weight, "replica", 1)
    shard_count = arrived.shape[1]
    span_cols = shard_count * piece_rows
    weight_part = arrived.transpose(1, 0, 2, 3).reshape(span_cols, rank_cols)
    projected = jnp.dot(spread, weight_part, preferred_element_type=jnp.float32)
    projected = projected.astype(jnp.bfloat16)
    kv_width = KCOLS // rank_count
    query_local = jnp.dot(tokens, query_weight, preferred_element_type=jnp.float32).astype(
        jnp.bfloat16
    )
    queries = lax.all_to_all(query_local, "section", split_axis=0, concat_axis=1, tiled=True)
    key_rows, value_rows = rows_first(
        (projected[:, :kv_width], projected[:, kv_width:]), "section", (1, 1)
    )
    block_rows = seq_len // rank_count
    positions = section_index * block_rows + jnp.arange(block_rows, dtype=jnp.int32)
    context = attend(queries, key_rows, value_rows, positions, lengths[0])
    return (new_master, new_first, new_second, context[None])


def solution(mesh):
    in_specs = (
        P("replica", "section", None),
        P("replica", None, None),
        P("replica"),
        P(None, "section"),
        P(None, "replica", None, "section"),
        P(None, "replica", None, "section"),
        P(None, "replica", None, "section"),
    )
    out_specs = (
        P(None, "replica", None, "section"),
        P(None, "replica", None, "section"),
        P(None, "replica", None, "section"),
        P("replica", "section", None),
    )
    return jax.shard_map(
        on_device, mesh=mesh, in_specs=in_specs, out_specs=out_specs, check_vma=False
    )
```

profile of v0, /device:TPU:130, one launch (start us, length us, event | category | flops | bytes accessed | tf_op | source)
XLA Modules:
  0.0 198.8 jit_solution(16823432170284284753)
XLA Ops:
  0.6 0.0 copy-start
  0.6 1.4 reshape.158
  2.1 74.1 %all_to_all.44 = bf16[64,5,1024]{2,1,0:T(8,128)(2,1)S(1)} all-to-all(bf16[64,5,1024]{2,1,0:T(8,128)(2,1)S(1)} %reshape.158), channel_id=1, replica_groups=mesh['section'=16,'replica'=64] {'replica'}, dimensions={0} | all-to-all | bytes 1310720 | tf_op jit(solution)/shard_map/all_to_all | solution.py:31
  76.2 0.2 convert_reduce_fusion
  76.4 0.1 reshape.160
  76.5 0.1 reshape.159
  76.6 0.1 pad_maximum_fusion
  76.7 0.3 copy.70
  76.9 0.5 broadcast.90
  77.4 1.9 reduce
  79.4 1.0 reshape.170
  80.4 8.6 %all-to-all-start.1 = ((f32[16,1,320]{2,1,0:T(1,128)}), f32[16,1,320]{2,1,0:T(1,128)S(1)}, u32[]{:S(2)}, u32[]{:S(2)}) async-start(f32[16,1,320]{2,1,0:T(1,128)} %reshape.170), calls=%async_computation.1 | async-start | bytes 49152 | tf_op jit(solution)/shard_map/all_to_all | solution.py:107
  89.0 0.0 copy-done
  89.0 0.0 copy-start.1
  89.0 0.0 copy-start.2
  89.0 0.0 copy-start.3
  89.0 2.8 %fusion.10 = bf16[256,160]{0,1:T(8,128)(2,1)S(1)} fusion(bf16[5120,160]{0,1:T(8,128)(2,1)S(1)} %copy-done, bf16[1,256,5120]{2,1,0:T(8,128)(2,1)} %param.8), kind=kOutput, calls=%fused_computation.13 | convolution fusion | flops 419471360 | bytes 4341760 | tf_op jit(solution)/shard_map/dot_general | solution.py:126
  91.8 0.8 copy.58
  92.6 3.6 %all-to-all-done.1 = f32[16,1,320]{2,1,0:T(1,128)S(1)} async-done(((f32[16,1,320]{2,1,0:T(1,128)}), f32[16,1,320]{2,1,0:T(1,128)S(1)}, u32[]{:S(2)}, u32[]{:S(2)}) %all-to-all-start.1) | async-done | bytes 20512 | tf_op jit(solution)/shard_map/all_to_all | solution.py:107
  96.1 4.8 %all-to-all-start.3 = ((bf16[16,16,160]{2,1,0:T(8,128)(2,1)}), bf16[16,16,160]{2,1,0:T(8,128)(2,1)S(1)}, u32[]{:S(2)}, u32[]{:S(2)}) async-start(bf16[16,16,160]{2,1,0:T(8,128)(2,1)} %bitcast.23), calls=%async_computation.3 | async-start | bytes 262144 | tf_op jit(solution)/shard_map/all_to_all | solution.py:129
  100.9 0.7 reduce.1
  101.6 0.9 reshape.171
  102.5 0.2 copy.71
  102.7 0.0 copy-done.1
  102.7 0.0 copy-done.2
  102.7 0.0 copy-done.3
  102.7 0.1 convert_bitcast_fusion
  102.8 0.2 broadcast_bitcast_fusion
  103.0 1.6 reshape.172
  104.6 4.0 %all-to-all-done.3 = bf16[16,16,160]{2,1,0:T(8,128)(2,1)S(1)} async-done(((bf16[16,16,160]{2,1,0:T(8,128)(2,1)}), bf16[16,16,160]{2,1,0:T(8,128)(2,1)S(1)}, u32[]{:S(2)}, u32[]{:S(2)}) %all-to-all-start.3) | async-done | bytes 81952 | tf_op jit(solution)/shard_map/all_to_all | solution.py:129
  108.6 7.0 %all-to-all-start.2 = ((bf16[64,2,2560]{2,1,0:T(2,128)(2,1)}), bf16[64,2,2560]{2,1,0:T(2,128)(2,1)}, u32[]{:S(2)}, u32[]{:S(2)}) async-start(bf16[64,2,2560]{2,1,0:T(2,128)(2,1)} %reshape.172), calls=%async_computation.2 | async-start | bytes 1310720 | tf_op jit(solution)/shard_map/all_to_all | solution.py:43
  115.5 4.4 %copy.56 = bf16[1,256,5120]{1,2,0:T(8,128)(2,1)} copy(bf16[1,256,5120]{2,1,0:T(8,128)(2,1)} %param.8) | data formatting | bytes 5242880 | tf_op args[1]
  119.9 6.0 %reshape_squeeze.3 = bf16[256,16,64,5]{0,3,2,1:T(8,128)(2,1)} reshape(bf16[1,256,5120]{1,2,0:T(8,128)(2,1)} %copy.56) | data formatting | bytes 5242880 | tf_op jit(solution)/shard_map/reshape;squeeze | solution.py:115
  126.7 0.1 fusion.32
  126.8 0.2 reshape.165
  127.0 0.7 copy.64
  127.6 0.7 copy.65
  128.3 0.7 copy.66
  129.0 24.7 %all-to-all-done.2 = bf16[64,2,2560]{2,1,0:T(2,128)(2,1)} async-done(((bf16[64,2,2560]{2,1,0:T(2,128)(2,1)}), bf16[64,2,2560]{2,1,0:T(2,128)(2,1)}, u32[]{:S(2)}, u32[]{:S(2)}) %all-to-all-start.2) | async-done | bytes 655392 | tf_op jit(solution)/shard_map/all_to_all | solution.py:43
  153.7 2.6 %reshape.173 = bf16[64,1,5,16,64]{4,3,2,1,0:T(8,128)(2,1)S(1)} reshape(bf16[64,2,2560]{2,1,0:T(2,128)(2,1)} %all-to-all-done.2) | data formatting | bytes 1310720
  156.2 1.9 copy.55
  158.1 3.4 %fusion.23 = bf16[256,64]{0,1:T(8,128)(2,1)S(1)} fusion(bf16[256,64,16,5]{0,3,1,2:T(8,128)(2,1)} %bitcast.84, bf16[64,16,1,5,64]{0,4,3,1,2:T(8,128)(2,1)} %copy.55), kind=kOutput, calls=%fused_computation.16 | convolution fusion | flops 167788544 | bytes 3309568 | tf_op jit(solution)/shard_map/dot_general | solution.py:123
  161.5 35.3 %all_gather.3 = bf16[512,512]{1,0:T(8,128)(2,1)S(1)} all-gather(bf16[32,512]{1,0:T(8,128)(2,1)S(1)} %pad_maximum_fusion.1), channel_id=1, replica_groups=mesh['section'=16,'replica'=64] {'section'}, dimensions={0}, use_global_device_ids=true | all-gather | bytes 557056 | tf_op jit(solution)/shard_map/all_gather | solution.py:55
  196.9 0.2 fusion.8
  197.1 0.2 fusion.38
  197.3 0.6 convolution_bitcast_fusion
  197.9 0.1 copy.63
  198.1 0.7 broadcast_select_fusion
  (9 shorter events, 0.2 us)
Async XLA Ops:
  0.6 88.3 %copy-start = (bf16[5120,160]{0,1:T(8,128)(2,1)S(1)}, bf16[5120,160]{0,1:T(8,128)(2,1)}, u32[]{:S(2)}) copy-start(bf16[5120,160]{0,1:T(8,128)(2,1)} %param.10) | copy-start | bytes 4915204
  80.4 15.8 %all-to-all-start.1 = ((f32[16,1,320]{2,1,0:T(1,128)}), f32[16,1,320]{2,1,0:T(1,128)S(1)}, u32[]{:S(2)}, u32[]{:S(2)}) async-start(f32[16,1,320]{2,1,0:T(1,128)} %reshape.170), calls=%async_computation.1 | async-start | bytes 49152 | tf_op jit(solution)/shard_map/all_to_all | solution.py:107
  89.0 13.7 %copy-start.1 = (f32[16,1,5,64]{3,1,2,0:T(1,128)S(1)}, f32[16,1,5,64]{3,1,2,0:T(1,128)}, u32[]{:S(2)}) copy-start(f32[16,1,5,64]{3,1,2,0:T(1,128)} %param.11) | copy-start | bytes 61444
  89.0 13.7 %copy-start.2 = (f32[16,1,5,64]{3,1,2,0:T(1,128)S(1)}, f32[16,1,5,64]{3,1,2,0:T(1,128)}, u32[]{:S(2)}) copy-start(f32[16,1,5,64]{3,1,2,0:T(1,128)} %param.12) | copy-start | bytes 61444
  89.0 13.7 %copy-start.3 = (f32[16,1,5,64]{3,1,2,0:T(1,128)S(1)}, f32[16,1,5,64]{3,1,2,0:T(1,128)}, u32[]{:S(2)}) copy-start(f32[16,1,5,64]{3,1,2,0:T(1,128)} %param.13) | copy-start | bytes 61444
  96.1 12.4 %all-to-all-start.3 = ((bf16[16,16,160]{2,1,0:T(8,128)(2,1)}), bf16[16,16,160]{2,1,0:T(8,128)(2,1)S(1)}, u32[]{:S(2)}, u32[]{:S(2)}) async-start(bf16[16,16,160]{2,1,0:T(8,128)(2,1)} %bitcast.23), calls=%async_computation.3 | async-start | bytes 262144 | tf_op jit(solution)/shard_map/all_to_all | solution.py:129
  108.6 45.1 %all-to-all-start.2 = ((bf16[64,2,2560]{2,1,0:T(2,128)(2,1)}), bf16[64,2,2560]{2,1,0:T(2,128)(2,1)}, u32[]{:S(2)}, u32[]{:S(2)}) async-start(bf16[64,2,2560]{2,1,0:T(2,128)(2,1)} %reshape.172), calls=%async_computation.2 | async-start | bytes 1310720 | tf_op jit(solution)/shard_map/all_to_all | solution.py:43
where the time goes:
time: 199 us
  blocking collectives  109 us (55%)
  waiting for transfers between devices  32.2 us (16%)
  local copies, waits for them, and re-layouts  24.3 us (12%)
  starting transfers between devices  20.3 us (10%)
  matrix products  6.96 us (3%)
  other arithmetic  4.06 us (2%)
    all_to_all x1, blocking collectives, sent_and_summed(): lax.all_to_all(blocks, axis, split_axis=0, concat_axis=0, tiled=True)  74.1 us
    all_gather x1, blocking collectives, rows_first(): filled, at, done = (lax.all_gather(both, axis, axis=0, tiled=True), 0, [])  35.3 us
    all_to_all x1, waiting for transfers between devices, copy_for_each(): lax.all_to_all(jnp.broadcast_to(array[None], (size, *array.shape)), axis,...  24.7 us
    unnamed x18, local copies, waits for them, and re-layouts  13.1 us
    all_to_all x1, starting transfers between devices, on_device(): lax.all_to_all(regrouped, 'section', split_axis=3, concat_axis=0, tiled=T...  8.58 us
    all_to_all x1, starting transfers between devices, copy_for_each(): lax.all_to_all(jnp.broadcast_to(array[None], (size, *array.shape)), axis,...  6.95 us
    another operation x1, local copies, waits for them, and re-layouts, on_device(): tokens.reshape(seq_len, rank_count, group_count, slab_rows)  6.04 us
    all_to_all x1, starting transfers between devices, on_device(): lax.all_to_all(query_local, 'section', split_axis=0, concat_axis=1, tiled...  4.77 us
  transfers between devices with their start and end apart: 3, of which 3 were waited for; matrix products, arithmetic and copies ran while one was open for 10% of the time, Pallas kernels for 0%

commit v1 on v0

v1 whole, which is shorter than its diff:
```python
import functools

import jax
import jax.numpy as jnp
from jax import lax
from jax.experimental import pallas as pl
from jax.experimental.pallas import tpu as pltpu
from jax.sharding import PartitionSpec as P

HEAD = 128
KV_HEADS = 4
GROUP = 5
QCOLS = 2560
KCOLS = 512
COLS = 1024
F32 = jnp.float32
BF16 = jnp.bfloat16
MESH = pl.DeviceIdType.MESH

BETA_ONE = 0.9
BETA_TWO = 0.95
EPSILON = 1e-08
DECAY = 0.1
RATE = 0.001
CORRECT_ONE = 1.0 - 0.9**50
CORRECT_TWO = 1.0 - 0.95**50


def adam_step(gradient, weight, first_moment, second_moment):
    new_first = BETA_ONE * first_moment + (1.0 - BETA_ONE) * gradient
    new_second = BETA_TWO * second_moment + (1.0 - BETA_TWO) * gradient * gradient
    direction = new_first / CORRECT_ONE / (jnp.sqrt(new_second / CORRECT_TWO) + EPSILON)
    new_master = weight - RATE * (direction + DECAY * weight)
    return (new_master, new_first, new_second)


def far_first(i):
    half = lax.div(i + 1, 2)
    return 8 + half * (1 - 2 * lax.rem(i, 2))


def near_first(i):
    return far_first(14 - i)


def update_kernel(
    g_hbm, hid_hbm, qw_hbm, ma_hbm, fm_hbm, sm_hbm,
    nm_ref, nf_ref, ns_ref, q_ref, proj_ref,
    gv, hv, qv, ma, fm, sm, ra, xs, rb, z32, zs, rz, sz, ss, rs, m2, agb, w2, w2b,
    lsem, asem_s, asem_r, bsem_s, bsem_r, zsem_s, zsem_r, ssem_s, ssem_r, gz_s, gx_s, gm_s, g_r,
):
    p = lax.axis_index("section")
    r = lax.axis_index("replica")
    core = lax.rem(r, 2)
    z = lax.rem(lax.div(r, 2), 16)
    xh = lax.div(r, 32)
    own_core = lax.div(p, 8)
    mate = r + 1 - 2 * core
    xmate = r + 32 - 64 * xh
    has_self = jnp.where(own_core == core, 1, 0)

    def zdev(zz):
        return xh * 32 + zz * 2 + core

    local = [
        pltpu.make_async_copy(src, dst, lsem.at[i])
        for i, (src, dst) in enumerate(
            ((g_hbm, gv), (hid_hbm, hv), (qw_hbm, qv), (ma_hbm, ma), (fm_hbm, fm), (sm_hbm, sm))
        )
    ]
    for copy in local:
        copy.start()

    barrier = pltpu.get_barrier_semaphore()

    def greet(section, replica):
        pl.semaphore_signal(
            barrier, inc=1, device_id={"section": section, "replica": replica}, device_id_type=MESH
        )

    greet(p, mate)
    greet(p, xmate)

    @pl.loop(0, 15)
    def _(i):
        greet(p, zdev(lax.rem(z + far_first(i), 16)))

    @pl.loop(0, 16)
    def _(i):
        @pl.when(jnp.logical_not(jnp.logical_and(i == p, own_core == core)))
        def _():
            greet(i, r - core + own_core)

    local[1].wait()
    local[2].wait()
    queries = lax.dot_general(hv[...], qv[...], (((1,), (1,)), ((), ())), preferred_element_type=F32)
    q_ref[...] = queries.astype(BF16)
    local[0].wait()
    pl.semaphore_wait(barrier, 33 - has_self)

    def remote(src, dst, send, recv, section, replica):
        return pltpu.make_async_remote_copy(
            src_ref=src, dst_ref=dst, send_sem=send, recv_sem=recv,
            device_id={"section": section, "replica": replica}, device_id_type=MESH,
        )

    theirs = pl.multiple_of((1 - core) * 256, 256)
    mine = pl.multiple_of(core * 256, 256)
    a_copies = [
        remote(gv.at[:, pl.ds(pl.multiple_of(theirs + side * 512, 256), 256)],
               ra.at[:, pl.ds(side * 256, 256)], asem_s.at[side], asem_r.at[side], p, mate)
        for side in range(2)
    ]
    for copy in a_copies:
        copy.start()
    for copy in a_copies:
        copy.wait_recv()

    def paired(row, side):
        own = gv[pl.ds(row, 16), pl.ds(pl.multiple_of(mine + side * 512, 256), 256)]
        return own.astype(F32) + ra[pl.ds(row, 16), pl.ds(side * 256, 256)].astype(F32)

    @pl.loop(0, 10)
    def _(ch):
        row = pl.multiple_of((1 - xh) * 160 + ch * 16, 16)
        for side in range(2):
            xs[pl.ds(pl.multiple_of(ch * 16, 16), 16), side * 256 : side * 256 + 256] = paired(row, side).astype(BF16)

    b_copy = remote(xs, rb, bsem_s, bsem_r, p, xmate)
    b_copy.start()
    b_copy.wait_recv()

    @pl.loop(0, 10)
    def _(ch):
        row = pl.multiple_of(xh * 160 + ch * 16, 16)
        part = pl.multiple_of(ch * 16, 16)
        for side in range(2):
            total = paired(row, side) + rb[pl.ds(part, 16), side * 256 : side * 256 + 256].astype(F32)
            for half in range(2):
                for tile in range(2):
                    z32[pl.ds(ch * 64 + half * 32 + side * 2 + tile, 8, stride=4), :] = total[
                        half * 8 : half * 8 + 8, tile * 128 : tile * 128 + 128
                    ]

    def z_copy(i):
        other = lax.rem(z + far_first(i), 16)
        return remote(zs.at[other], rz.at[z], zsem_s.at[i], zsem_r.at[z], p, zdev(other))

    @pl.loop(0, 15)
    def _(i):
        other = lax.rem(z + far_first(i), 16)
        piece = z32[pl.ds(pl.multiple_of(other * 40, 8), 40), :]
        zs[other] = piece.astype(BF16).reshape(5, 8, 128)
        z_copy(i).start()

    sz[0:40, :] = z32[pl.ds(pl.multiple_of(z * 40, 8), 40), :]
    sz[40:64, :] = jnp.zeros((24, 128), F32)

    @pl.loop(0, 15)
    def _(i):
        other = lax.rem(z + near_first(i), 16)
        remote(zs.at[other], rz.at[other], zsem_s.at[i], zsem_r.at[other], p, zdev(other)).wait_recv()
        sz[0:40, :] += rz[other].astype(F32).reshape(40, 128)

    lane = lax.broadcasted_iota(jnp.int32, (8, 128), 1)
    for cc in range(2):
        for quad in range(2):
            keys = sz[pl.ds(cc * 20 + quad, 8, stride=4), :]
            values = sz[pl.ds(cc * 20 + 2 + quad, 8, stride=4), :]
            for j in range(4):
                key_part = pltpu.roll(keys, (128 - 32 * j) % 128, 1) if j else keys
                value_part = pltpu.roll(values, (160 - 32 * j) % 128, 1) if j != 1 else values
                ss[cc * 8 + quad * 4 + j] = jnp.where(lane < 32, key_part, value_part)

    def s_copy(i):
        section = core * 8 + lax.rem(i, 8)
        return remote(ss.at[i], rs.at[p], ssem_s.at[i], ssem_r.at[p], section, r - core + lax.div(i, 8))

    def s_here(i):
        return jnp.logical_and(core * 8 + lax.rem(i, 8) == p, lax.div(i, 8) == core)

    @pl.loop(0, 16)
    def _(i):
        @pl.when(jnp.logical_not(s_here(i)))
        def _():
            s_copy(i).start()

    @pl.when(own_core == core)
    def _():
        rs[p] = ss[core * 8 + lax.rem(p, 8)]

    for copy in local[3:]:
        copy.wait()

    @pl.loop(0, 16)
    def _(i):
        @pl.when(jnp.logical_not(jnp.logical_and(i == p, own_core == core)))
        def _():
            remote(ss.at[i], rs.at[i], ssem_s.at[i], ssem_r.at[i], i, r - core + own_core).wait_recv()

    @pl.loop(0, 16)
    def _(i):
        rows = pl.ds(i * 5, 5)
        new_master, new_first, new_second = adam_step(
            rs[i, 0:5, 0:64], ma[rows, 0, :], fm[rows, 0, :], sm[rows, 0, :]
        )
        nm_ref[rows, 0, :] = new_master
        nf_ref[rows, 0, :] = new_first
        ns_ref[rows, 0, :] = new_second
        rs[i, 0:5, 0:64] = new_master

    for i in range(8):
        m2[i * 8 : i * 8 + 8, :] = jnp.where(lane < 64, rs[i], pltpu.roll(rs[i + 8], 64, 1))
    for k in range(5):
        agb[r, k] = m2[pl.ds(k, 8, stride=8), :].astype(BF16)

    def gz_copy(i):
        return remote(agb.at[r], agb.at[r], gz_s.at[i], g_r.at[r], p, zdev(lax.rem(z + far_first(i), 16)))

    def gx_copy(i, slot):
        return remote(agb.at[slot], agb.at[slot], gx_s.at[i], g_r.at[slot], p, xmate)

    def gm_copy(i, slot):
        return remote(agb.at[slot], agb.at[slot], gm_s.at[i], g_r.at[slot], p, mate)

    def arrive(slot):
        remote(agb.at[slot], agb.at[slot], gm_s.at[0], g_r.at[slot], p, mate).wait_recv()

    def scatter(slot):
        for k in range(5):
            w2[pl.ds(slot * 5 + k, 8, stride=320), :] = agb[slot, k].astype(F32)

    @pl.loop(0, 15)
    def _(i):
        gz_copy(i).start()

    gx_copy(15, r).start()
    gm_copy(31, r).start()
    scatter(r)

    @pl.loop(0, 15)
    def _(i):
        slot = zdev(lax.rem(z + near_first(i), 16))
        arrive(slot)
        gx_copy(i, slot).start()
        gm_copy(i, slot).start()
        scatter(slot)

    def xslot(i):
        far = jnp.where(i == 0, 0, near_first(i - 1))
        return (1 - xh) * 32 + lax.rem(z + far, 16) * 2 + core

    @pl.loop(0, 16)
    def _(i):
        slot = xslot(i)
        arrive(slot)
        gm_copy(15 + i, slot).start()
        scatter(slot)

    @pl.loop(0, 32)
    def _(i):
        slot = i * 2 + 1 - core
        arrive(slot)
        scatter(slot)

    w2b[...] = w2[...].astype(BF16)
    low = jnp.dot(hv[:, :2560], w2b[...], preferred_element_type=F32)
    high = jnp.dot(hv[:, 2560:], w2b[...], preferred_element_type=F32)
    proj_ref[...] = (low[:, :64] + high[:, 64:]).astype(BF16)

    for copy in a_copies:
        copy.wait_send()
    b_copy.wait_send()

    @pl.loop(0, 15)
    def _(i):
        z_copy(i).wait_send()
        gz_copy(i).wait_send()
        gx_copy(i, zdev(lax.rem(z + near_first(i), 16))).wait_send()
        gm_copy(i, zdev(lax.rem(z + near_first(i), 16))).wait_send()

    gx_copy(15, r).wait_send()
    gm_copy(31, r).wait_send()

    @pl.loop(0, 16)
    def _(i):
        gm_copy(15 + i, xslot(i)).wait_send()

        @pl.when(jnp.logical_not(s_here(i)))
        def _():
            s_copy(i).wait_send()


def update(gradients, tokens, query_weight_t, master, first, second):
    vm = pltpu.VMEM
    dma = pltpu.SemaphoreType.DMA
    state = jax.ShapeDtypeStruct((80, 1, 64), F32)
    anyspace = pl.BlockSpec(memory_space=pl.ANY)
    vmem = pl.BlockSpec(memory_space=pltpu.VMEM)
    return pl.pallas_call(
        update_kernel,
        out_shape=(
            state, state, state,
            jax.ShapeDtypeStruct((256, 160), BF16),
            jax.ShapeDtypeStruct((256, 64), BF16),
        ),
        in_specs=[anyspace] * 6,
        out_specs=(vmem,) * 5,
        scratch_shapes=[
            vm((320, 1024), BF16),
            vm((256, 5120), BF16),
            vm((160, 5120), BF16),
            vm((80, 1, 64), F32), vm((80, 1, 64), F32), vm((80, 1, 64), F32),
            vm((320, 512), BF16),
            vm((160, 512), BF16),
            vm((160, 512), BF16),
            vm((640, 128), F32),
            vm((16, 5, 8, 128), BF16),
            vm((16, 5, 8, 128), BF16),
            vm((64, 128), F32),
            vm((16, 8, 128), F32),
            vm((16, 8, 128), F32),
            vm((64, 128), F32),
            vm((64, 5, 8, 128), BF16),
            vm((2560, 128), F32),
            vm((2560, 128), BF16),
            dma((6,)), dma((2,)), dma((2,)), dma, dma, dma((15,)), dma((16,)),
            dma((16,)), dma((16,)), dma((15,)), dma((16,)), dma((32,)), dma((64,)),
        ],
        compiler_params=pltpu.CompilerParams(collective_id=0, has_side_effects=True),
        name="update",
    )(gradients, tokens, query_weight_t, master, first, second)


def rows_first(arrays, axis, dims):
    turned = [jnp.moveaxis(a, dim, 0) for a, dim in zip(arrays, dims)]
    both = jnp.concatenate([t.reshape(len(t), -1) for t in turned], axis=1)
    filled, at, done = (lax.all_gather(both, axis, axis=0, tiled=True), 0, [])
    for t, dim in zip(turned, dims):
        section = filled[:, at : at + t[0].size].reshape(-1, *t.shape[1:])
        done.append(jnp.moveaxis(section, 0, dim))
        at += t[0].size
    return tuple(done)


def attend(queries, key_rows, value_rows, positions, length):
    query_count = queries.shape[0]
    seq_len = key_rows.shape[0]
    grouped = queries.reshape(query_count, KV_HEADS, GROUP, HEAD)
    key_heads = key_rows.reshape(seq_len, KV_HEADS, HEAD)
    value_heads = value_rows.reshape(seq_len, KV_HEADS, HEAD)
    scores = jnp.einsum(
        "tkgd,jkd->kgtj", grouped, key_heads, preferred_element_type=jnp.float32
    ) * HEAD ** (-0.5)
    key_pos = jnp.arange(seq_len, dtype=jnp.int32)
    allowed = (key_pos[None, :] <= positions[:, None]) & (key_pos[None, :] < length)
    scores = jnp.where(allowed[None, None], scores, -jnp.inf)
    row_max = jnp.max(scores, axis=-1, keepdims=True)
    expo = jnp.exp(scores - row_max)
    probs = (expo / jnp.sum(expo, axis=-1, keepdims=True)).astype(jnp.bfloat16)
    mixed = jnp.einsum("kgtj,jkd->tkgd", probs, value_heads, preferred_element_type=jnp.float32)
    mixed = mixed.reshape(query_count, QCOLS)
    live_rows = positions < length
    return jnp.where(live_rows[:, None], mixed, 0.0)


def on_device(gradients, hidden, lengths, query_weight, master, first_moment, second_moment):
    rank_count = lax.axis_size("section")
    section_index = lax.axis_index("section")
    seq_len = hidden.shape[1]
    states = [a.reshape(80, 1, 64) for a in (master, first_moment, second_moment)]
    new_master, new_first, new_second, query_local, projected = update(
        gradients[0], hidden[0], query_weight.T, *states
    )
    kv_width = KCOLS // rank_count
    queries = lax.all_to_all(query_local, "section", split_axis=0, concat_axis=1, tiled=True)
    key_rows, value_rows = rows_first(
        (projected[:, :kv_width], projected[:, kv_width:]), "section", (1, 1)
    )
    block_rows = seq_len // rank_count
    positions = section_index * block_rows + jnp.arange(block_rows, dtype=jnp.int32)
    context = attend(queries, key_rows, value_rows, positions, lengths[0])
    back = [a.reshape(16, 1, 5, 64) for a in (new_master, new_first, new_second)]
    return (*back, context[None])


def solution(mesh):
    in_specs = (
        P("replica", "section", None),
        P("replica", None, None),
        P("replica"),
        P(None, "section"),
        P(None, "replica", None, "section"),
        P(None, "replica", None, "section"),
        P(None, "replica", None, "section"),
    )
    out_specs = (
        P(None, "replica", None, "section"),
        P(None, "replica", None, "section"),
        P(None, "replica", None, "section"),
        P("replica", "section", None),
    )
    return jax.shard_map(
        on_device, mesh=mesh, in_specs=in_specs, out_specs=out_specs, check_vma=False
    )
```

time: 199 us -> 114 us (0.57)
  the two profiles are of different devices: /device:TPU:130 before, /device:TPU:2 now
where the time goes in v1:
time: 114 us; the launch traced here: 113 us
  Pallas kernels  63.9 us (56%)
  blocking collectives  35.2 us (31%)
  starting transfers between devices  7.49 us (7%)
  local copies, waits for them, and re-layouts  3.39 us (3%)
  between operations  1.38 us (1%)
    pallas_call x1, Pallas kernels, update(): pl.pallas_call(update_kernel, out_shape=(state, state, state, jax.ShapeDt...  63.9 us
    all_gather x1, blocking collectives, rows_first(): filled, at, done = (lax.all_gather(both, axis, axis=0, tiled=True), 0, [])  35.2 us
    all_to_all x1, starting transfers between devices, on_device(): lax.all_to_all(query_local, 'section', split_axis=0, concat_axis=1, tiled...  7.49 us
  transfers between devices with their start and end apart: 1, of which 0 were waited for; matrix products, arithmetic and copies ran while one was open for 1% of the time, Pallas kernels for 0%

profile of v1, /device:TPU:2, one launch (start us, length us, event | category | flops | bytes accessed | tf_op | source)
XLA Modules:
  0.0 113.3 jit_solution(11649958705886824888)
XLA Ops:
  0.6 63.9 %update.1 = (f32[80,1,64]{2,1,0:T(1,128)}, f32[80,1,64]{2,1,0:T(1,128)}, f32[80,1,64]{2,1,0:T(1,128)}, bf16[256,160]{1,0:T(8,128)(2,1)}, bf16[256,64]{1,0:T(8,128)(2,1)}) custom-call(bf16[320,1024]{1,0:T(8,128)(2,1)} %bitcast.45, bf16[256,5120]{1,0:T(8,128)(2,1)} %bitcast.42, bf16[160,5120]{1,0:T(8,128)(2,1)} %bitcast.43, f32[80,1,64]{2,1,0:T(1,128)} %bitcast.49, ...), custom_call_target="tpu_custom_call" | custom-call | tf_op jit(solution)/shard_map/update/pallas_call | solution.py:300
  64.6 7.5 %all-to-all-start = ((bf16[16,16,160]{2,1,0:T(8,128)(2,1)}), bf16[16,16,160]{2,1,0:T(8,128)(2,1)S(1)}, u32[]{:S(2)}, u32[]{:S(2)}) async-start(bf16[16,16,160]{2,1,0:T(8,128)(2,1)} %bitcast.48), calls=%async_computation | async-start | bytes 262144 | tf_op jit(solution)/shard_map/all_to_all | solution.py:376
  72.0 1.0 slice_bitcast_fusion.1
  73.0 0.1 copy.23
  73.1 0.1 copy.24
  73.2 35.2 %all_gather.3 = bf16[512,512]{1,0:T(8,128)(2,1)S(1)} all-gather(bf16[32,512]{1,0:T(8,128)(2,1)S(1)} %pad_maximum_fusion), channel_id=1, replica_groups=mesh['section'=16,'replica'=64] {'section'}, dimensions={0}, use_global_device_ids=true | all-gather | bytes 557056 | tf_op jit(solution)/shard_map/all_gather | solution.py:338
  108.4 0.0 copy-start.2
  108.4 0.0 copy-start.1
  108.4 0.0 copy-start
  109.1 0.1 fusion.7
  109.2 0.0 all-to-all-done
  109.3 0.2 reshape.127
  109.5 0.2 fusion.3
  109.7 0.2 fusion.10
  109.9 0.6 convolution_bitcast_fusion
  110.5 0.1 copy.29
  110.7 0.7 broadcast_select_fusion
  111.4 0.0 copy-done.2
  111.4 0.6 copy.42
  112.0 0.0 copy-done.1
  112.0 0.6 copy.43
  112.6 0.0 copy-done
  112.7 0.6 copy.44
  (7 shorter events, 0.2 us)
Async XLA Ops:
  64.6 44.7 %all-to-all-start = ((bf16[16,16,160]{2,1,0:T(8,128)(2,1)}), bf16[16,16,160]{2,1,0:T(8,128)(2,1)S(1)}, u32[]{:S(2)}, u32[]{:S(2)}) async-start(bf16[16,16,160]{2,1,0:T(8,128)(2,1)} %bitcast.48), calls=%async_computation | async-start | bytes 262144 | tf_op jit(solution)/shard_map/all_to_all | solution.py:376
  108.4 3.0 %copy-start.2 = (f32[80,1,64]{2,1,0:T(1,128)S(1)}, f32[80,1,64]{2,1,0:T(1,128)}, u32[]{:S(2)}) copy-start(f32[80,1,64]{2,1,0:T(1,128)} %get-tuple-element.9) | copy-start | bytes 61444
  108.4 3.6 %copy-start.1 = (f32[80,1,64]{2,1,0:T(1,128)S(1)}, f32[80,1,64]{2,1,0:T(1,128)}, u32[]{:S(2)}) copy-start(f32[80,1,64]{2,1,0:T(1,128)} %get-tuple-element.10) | copy-start | bytes 61444
  108.4 4.2 %copy-start = (f32[80,1,64]{2,1,0:T(1,128)S(1)}, f32[80,1,64]{2,1,0:T(1,128)}, u32[]{:S(2)}) copy-start(f32[80,1,64]{2,1,0:T(1,128)} %get-tuple-element.11) | copy-start | bytes 61444

commit v2 on v1

--- a/solution.py
+++ b/solution.py
@@ -8,11 +8,8 @@
 from jax.sharding import PartitionSpec as P
 
 HEAD = 128
-KV_HEADS = 4
 GROUP = 5
 QCOLS = 2560
-KCOLS = 512
-COLS = 1024
 F32 = jnp.float32
 BF16 = jnp.bfloat16
 MESH = pl.DeviceIdType.MESH
@@ -44,10 +41,12 @@
 
 
 def update_kernel(
-    g_hbm, hid_hbm, qw_hbm, ma_hbm, fm_hbm, sm_hbm,
-    nm_ref, nf_ref, ns_ref, q_ref, proj_ref,
+    g_hbm, hid_hbm, qw_hbm, ma_hbm, fm_hbm, sm_hbm, len_ref,
+    nm_ref, nf_ref, ns_ref, ctx_ref,
     gv, hv, qv, ma, fm, sm, ra, xs, rb, z32, zs, rz, sz, ss, rs, m2, agb, w2, w2b,
+    qs, qr, qall, kvs, kvr, keys_all, values_all, cs, cr,
     lsem, asem_s, asem_r, bsem_s, bsem_r, zsem_s, zsem_r, ssem_s, ssem_r, gz_s, gx_s, gm_s, g_r,
+    qsem_s, qsem_r, ksem_s, ksem_r, csem_s, csem_r,
 ):
     p = lax.axis_index("section")
     r = lax.axis_index("replica")
@@ -58,6 +57,8 @@
     mate = r + 1 - 2 * core
     xmate = r + 32 - 64 * xh
     has_self = jnp.where(own_core == core, 1, 0)
+    kv_head = lax.div(p, 4)
+    quarter = lax.rem(p, 4)
 
     def zdev(zz):
         return xh * 32 + zz * 2 + core
@@ -91,12 +92,20 @@
         def _():
             greet(i, r - core + own_core)
 
+    @pl.loop(1, 4)
+    def _(i):
+        greet(kv_head * 4 + lax.rem(quarter + i, 4), r)
+        greet(lax.rem(kv_head + i, 4) * 4 + quarter, r)
+
     local[1].wait()
     local[2].wait()
     queries = lax.dot_general(hv[...], qv[...], (((1,), (1,)), ((), ())), preferred_element_type=F32)
-    q_ref[...] = queries.astype(BF16)
+    queries = queries.astype(BF16)
+    for j in range(4):
+        for m in range(4):
+            qs[j, m * 16 : m * 16 + 16, 0:160] = queries[m * 64 + j * 16 : m * 64 + j * 16 + 16]
     local[0].wait()
-    pl.semaphore_wait(barrier, 33 - has_self)
+    pl.semaphore_wait(barrier, 39 - has_self)
 
     def remote(src, dst, send, recv, section, replica):
         return pltpu.make_async_remote_copy(
@@ -113,6 +122,16 @@
     ]
     for copy in a_copies:
         copy.start()
+
+    def q_copy(i):
+        other = lax.rem(quarter + i, 4)
+        return remote(qs.at[other], qr.at[quarter], qsem_s.at[i], qsem_r.at[quarter], kv_head * 4 + other, r)
+
+    @pl.loop(1, 4)
+    def _(i):
+        q_copy(i).start()
+
+    qr[quarter] = qs[quarter]
     for copy in a_copies:
         copy.wait_recv()
 
@@ -153,6 +172,14 @@
         zs[other] = piece.astype(BF16).reshape(5, 8, 128)
         z_copy(i).start()
 
+    @pl.loop(1, 4)
+    def _(i):
+        other = lax.rem(quarter + i, 4)
+        remote(qs.at[other], qr.at[other], qsem_s.at[i], qsem_r.at[other], kv_head * 4 + other, r).wait_recv()
+
+    for j in range(4):
+        qall[:, j * 160 : j * 160 + 160] = qr[j, :, 0:160]
+
     sz[0:40, :] = z32[pl.ds(pl.multiple_of(z * 40, 8), 40), :]
     sz[40:64, :] = jnp.zeros((24, 128), F32)
 
@@ -266,11 +293,84 @@
     w2b[...] = w2[...].astype(BF16)
     low = jnp.dot(hv[:, :2560], w2b[...], preferred_element_type=F32)
     high = jnp.dot(hv[:, 2560:], w2b[...], preferred_element_type=F32)
-    proj_ref[...] = (low[:, :64] + high[:, 64:]).astype(BF16)
+    wide = lax.broadcasted_iota(jnp.int32, (128, 128), 1)
+    first = low[:128] + pltpu.roll(high[:128], 64, 1)
+    second = pltpu.roll(low[128:], 64, 1) + high[128:]
+    both = jnp.where(wide < 64, first, second)
+    kvs[...] = pltpu.roll(both, quarter * 32, 1).astype(BF16)
+
+    def k_copy(i):
+        return remote(
+            kvs, kvr.at[quarter], ksem_s.at[i], ksem_r.at[quarter], kv_head * 4 + lax.rem(quarter + i, 4), r
+        )
+
+    @pl.loop(1, 4)
+    def _(i):
+        k_copy(i).start()
+
+    kvr[quarter] = kvs[...]
+
+    @pl.loop(1, 4)
+    def _(i):
+        other = lax.rem(quarter + i, 4)
+        remote(kvs, kvr.at[other], ksem_s.at[i], ksem_r.at[other], kv_head * 4 + other, r).wait_recv()
+
+    block = lax.div(wide, 32)
+    for turn in range(4):
+        merged = kvr[(3 - turn) % 4].astype(F32)
+        for j in range(4):
+            if (j + turn) % 4 != 3:
+                merged = jnp.where(block == (j + turn) % 4, kvr[j].astype(F32), merged)
+        if turn:
+            merged = pltpu.roll(merged, 128 - 32 * turn, 1)
+        dest = values_all if turn % 2 else keys_all
+        dest[(turn // 2) * 128 : (turn // 2) * 128 + 128, :] = merged.astype(BF16)
+
+    token = lax.broadcasted_iota(jnp.int32, (64, 256), 0)
+    position = lax.div(token, 16) * 64 + lax.rem(token, 16) + quarter * 16
+    key_pos = lax.broadcasted_iota(jnp.int32, (64, 256), 1)
+    length = len_ref[0]
+    allowed = jnp.logical_and(key_pos <= position, key_pos < length)
+    live = position[:, :128] < length
+    for h in range(GROUP):
+        scores = lax.dot_general(
+            qall[:, h * 128 : h * 128 + 128], keys_all[...], (((1,), (1,)), ((), ())), preferred_element_type=F32
+        )
+        scores = jnp.where(allowed, scores * HEAD ** (-0.5), -jnp.inf)
+        expo = jnp.exp(scores - jnp.max(scores, axis=1, keepdims=True))
+        probs = (expo / jnp.sum(expo, axis=1, keepdims=True)).astype(BF16)
+        mixed = jnp.dot(probs, values_all[...], preferred_element_type=F32)
+        mixed = jnp.where(live, mixed, 0.0).astype(BF16)
+        for m in range(4):
+            cs[m, :, h * 128 : h * 128 + 128] = mixed[m * 16 : m * 16 + 16]
+
+    def c_copy(i):
+        other = lax.rem(kv_head + i, 4)
+        return remote(cs.at[other], cr.at[kv_head], csem_s.at[i], csem_r.at[kv_head], other * 4 + quarter, r)
+
+    @pl.loop(1, 4)
+    def _(i):
+        c_copy(i).start()
+
+    cr[kv_head] = cs[kv_head]
+
+    @pl.loop(1, 4)
+    def _(i):
+        other = lax.rem(kv_head + i, 4)
+        remote(cs.at[other], cr.at[other], csem_s.at[i], csem_r.at[other], other * 4 + quarter, r).wait_recv()
+
+    for m in range(4):
+        ctx_ref[:, m * 640 : m * 640 + 640] = cr[m].astype(F32)
 
     for copy in a_copies:
         copy.wait_send()
     b_copy.wait_send()
+
+    @pl.loop(1, 4)
+    def _(i):
+        q_copy(i).wait_send()
+        k_copy(i).wait_send()
+        c_copy(i).wait_send()
 
     @pl.loop(0, 15)
     def _(i):
@@ -291,7 +391,7 @@
             s_copy(i).wait_send()
 
 
-def update(gradients, tokens, query_weight_t, master, first, second):
+def update(gradients, tokens, query_weight_t, master, first, second, lengths):
     vm = pltpu.VMEM
     dma = pltpu.SemaphoreType.DMA
     state = jax.ShapeDtypeStruct((80, 1, 64), F32)
@@ -301,11 +401,10 @@
         update_kernel,
         out_shape=(
             state, state, state,
-            jax.ShapeDtypeStruct((256, 160), BF16),
-            jax.ShapeDtypeStruct((256, 64), BF16),
+            jax.ShapeDtypeStruct((16, QCOLS), F32),
         ),
-        in_specs=[anyspace] * 6,
-        out_specs=(vmem,) * 5,
+        in_specs=[anyspace] * 6 + [pl.BlockSpec(memory_space=pltpu.SMEM)],
+        out_specs=(vmem,) * 4,
         scratch_shapes=[
             vm((320, 1024), BF16),
             vm((256, 5120), BF16),
@@ -324,64 +423,28 @@
             vm((64, 5, 8, 128), BF16),
             vm((2560, 128), F32),
             vm((2560, 128), BF16),
+            vm((4, 64, 256), BF16),
+            vm((4, 64, 256), BF16),
+            vm((64, 640), BF16),
+            vm((128, 128), BF16),
+            vm((4, 128, 128), BF16),
+            vm((256, 128), BF16),
+            vm((256, 128), BF16),
+            vm((4, 16, 640), BF16),
+            vm((4, 16, 640), BF16),
             dma((6,)), dma((2,)), dma((2,)), dma, dma, dma((15,)), dma((16,)),
             dma((16,)), dma((16,)), dma((15,)), dma((16,)), dma((32,)), dma((64,)),
+            dma((4,)), dma((4,)), dma((4,)), dma((4,)), dma((4,)), dma((4,)),
         ],
         compiler_params=pltpu.CompilerParams(collective_id=0, has_side_effects=True),
         name="update",
-    )(gradients, tokens, query_weight_t, master, first, second)
-
-
-def rows_first(arrays, axis, dims):
-    turned = [jnp.moveaxis(a, dim, 0) for a, dim in zip(arrays, dims)]
-    both = jnp.concatenate([t.reshape(len(t), -1) for t in turned], axis=1)
-    filled, at, done = (lax.all_gather(both, axis, axis=0, tiled=True), 0, [])
-    for t, dim in zip(turned, dims):
-        section = filled[:, at : at + t[0].size].reshape(-1, *t.shape[1:])
-        done.append(jnp.moveaxis(section, 0, dim))
-        at += t[0].size
-    return tuple(done)
-
-
-def attend(queries, key_rows, value_rows, positions, length):
-    query_count = queries.shape[0]
-    seq_len = key_rows.shape[0]
-    grouped = queries.reshape(query_count, KV_HEADS, GROUP, HEAD)
-    key_heads = key_rows.reshape(seq_len, KV_HEADS, HEAD)
-    value_heads = value_rows.reshape(seq_len, KV_HEADS, HEAD)
-    scores = jnp.einsum(
-        "tkgd,jkd->kgtj", grouped, key_heads, preferred_element_type=jnp.float32
-    ) * HEAD ** (-0.5)
-    key_pos = jnp.arange(seq_len, dtype=jnp.int32)
-    allowed = (key_pos[None, :] <= positions[:, None]) & (key_pos[None, :] < length)
-    scores = jnp.where(allowed[None, None], scores, -jnp.inf)
-    row_max = jnp.max(scores, axis=-1, keepdims=True)
-    expo = jnp.exp(scores - row_max)
-    probs = (expo / jnp.sum(expo, axis=-1, keepdims=True)).astype(jnp.bfloat16)
-    mixed = jnp.einsum("kgtj,jkd->tkgd", probs, value_heads, preferred_element_type=jnp.float32)
-    mixed = mixed.reshape(query_count, QCOLS)
-    live_rows = positions < length
-    return jnp.where(live_rows[:, None], mixed, 0.0)
+    )(gradients, tokens, query_weight_t, master, first, second, lengths)
 
 
 def on_device(gradients, hidden, lengths, query_weight, master, first_moment, second_moment):
-    rank_count = lax.axis_size("section")
-    section_index = lax.axis_index("section")
-    seq_len = hidden.shape[1]
     states = [a.reshape(80, 1, 64) for a in (master, first_moment, second_moment)]
-    new_master, new_first, new_second, query_local, projected = update(
-        gradients[0], hidden[0], query_weight.T, *states
-    )
-    kv_width = KCOLS // rank_count
-    queries = lax.all_to_all(query_local, "section", split_axis=0, concat_axis=1, tiled=True)
-    key_rows, value_rows = rows_first(
-        (projected[:, :kv_width], projected[:, kv_width:]), "section", (1, 1)
-    )
-    block_rows = seq_len // rank_count
-    positions = section_index * block_rows + jnp.arange(block_rows, dtype=jnp.int32)
-    context = attend(queries, key_rows, value_rows, positions, lengths[0])
-    back = [a.reshape(16, 1, 5, 64) for a in (new_master, new_first, new_second)]
-    return (*back, context[None])
+    *states, context = update(gradients[0], hidden[0], query_weight.T, *states, lengths)
+    return (*[a.reshape(16, 1, 5, 64) for a in states], context[None])
 
 
 def solution(mesh):

time: 114 us -> 85.5 us (0.75)
  the two profiles are of different devices: /device:TPU:2 before, /device:TPU:1 now
where the time goes in v2:
time: 85.5 us; the launch traced here: 84.7 us
  Pallas kernels  77.6 us (91%)
  local copies, waits for them, and re-layouts  5.81 us (7%)
  between operations  1.29 us (2%)
    pallas_call x1, Pallas kernels, update(): pl.pallas_call(update_kernel, out_shape=(state, state, state, jax.ShapeDt...  77.6 us
    unnamed x4, local copies, waits for them, and re-layouts  5.81 us

profile of v2, /device:TPU:1, one launch (start us, length us, event | category | flops | bytes accessed | tf_op | source)
XLA Modules:
  0.0 84.7 jit_solution(4111261946399713920)
XLA Ops:
  1.3 77.6 %update.1 = (f32[80,1,64]{2,1,0:T(1,128)}, f32[80,1,64]{2,1,0:T(1,128)}, f32[80,1,64]{2,1,0:T(1,128)}, f32[16,2560]{1,0:T(8,128)}) custom-call(bf16[320,1024]{1,0:T(8,128)(2,1)} %bitcast.12, bf16[256,5120]{1,0:T(8,128)(2,1)} %bitcast.10, bf16[160,5120]{1,0:T(8,128)(2,1)} %bitcast.11, f32[80,1,64]{2,1,0:T(1,128)} %bitcast.17, f32[80,1,64]{2,1,0:T(1,128)} %bitcast.18, ...), custom_call_target="tpu_custom_call" | custom-call | tf_op jit(solution)/shard_map/update/pallas_call | solution.py:400
  78.9 1.4 %copy.16 = f32[16,1,5,64]{3,1,2,0:T(1,128)} copy(f32[16,1,5,64]{3,1,2,0:T(1,128)} %bitcast.16) | data formatting | bytes 40960
  80.3 1.4 %copy.17 = f32[16,1,5,64]{3,1,2,0:T(1,128)} copy(f32[16,1,5,64]{3,1,2,0:T(1,128)} %bitcast.15) | data formatting | bytes 40960
  81.7 1.4 %copy.18 = f32[16,1,5,64]{3,1,2,0:T(1,128)} copy(f32[16,1,5,64]{3,1,2,0:T(1,128)} %bitcast.14) | data formatting | bytes 40960
  83.2 1.6 %copy.19 = f32[1,16,2560]{2,1,0:T(8,128)} copy(f32[1,16,2560]{2,1,0:T(8,128)} %bitcast.13) | data formatting | bytes 327680

commit v3 on v2

--- a/solution.py
+++ b/solution.py
@@ -43,9 +43,9 @@
 def update_kernel(
     g_hbm, hid_hbm, qw_hbm, ma_hbm, fm_hbm, sm_hbm, len_ref,
     nm_ref, nf_ref, ns_ref, ctx_ref,
-    gv, hv, qv, ma, fm, sm, ra, xs, rb, z32, zs, rz, sz, ss, rs, m2, agb, w2, w2b,
+    gv, hv, qv, ma, fm, sm, ra, xo32, xs, xr, z32, zs, rz, sz, ss, rs, m2, agb, w2, w2b,
     qs, qr, qall, kvs, kvr, keys_all, values_all, cs, cr,
-    lsem, asem_s, asem_r, bsem_s, bsem_r, zsem_s, zsem_r, ssem_s, ssem_r, gz_s, gx_s, gm_s, g_r,
+    lsem, asem_s, asem_r, xsem_s, xsem_r, zsem_s, zsem_r, ssem_s, ssem_r, gz_s, gx_s, gm_s, g_r,
     qsem_s, qsem_r, ksem_s, ksem_r, csem_s, csem_r,
 ):
     p = lax.axis_index("section")
@@ -59,6 +59,7 @@
     has_self = jnp.where(own_core == core, 1, 0)
     kv_head = lax.div(p, 4)
     quarter = lax.rem(p, 4)
+    served = lax.rem(p + 2, 4)
 
     def zdev(zz):
         return xh * 32 + zz * 2 + core
@@ -95,7 +96,80 @@
     @pl.loop(1, 4)
     def _(i):
         greet(kv_head * 4 + lax.rem(quarter + i, 4), r)
-        greet(lax.rem(kv_head + i, 4) * 4 + quarter, r)
+
+    @pl.loop(0, 4)
+    def _(i):
+        greet(i * 4 + served, r)
+
+    local[0].wait()
+    pl.semaphore_wait(barrier, 40 - has_self)
+
+    def remote(src, dst, send, recv, section, replica):
+        return pltpu.make_async_remote_copy(
+            src_ref=src, dst_ref=dst, send_sem=send, recv_sem=recv,
+            device_id={"section": section, "replica": replica}, device_id_type=MESH,
+        )
+
+    theirs = pl.multiple_of((1 - core) * 256, 256)
+    mine = pl.multiple_of(core * 256, 256)
+    a_copies = [
+        remote(gv.at[pl.ds(row, 160), pl.ds(pl.multiple_of(theirs + side * 512, 256), 256)],
+               ra.at[pl.ds(row, 160), pl.ds(side * 256, 256)],
+               asem_s.at[turn * 2 + side], asem_r.at[turn * 2 + side], p, mate)
+        for turn, row in enumerate((pl.multiple_of((1 - xh) * 160, 16), pl.multiple_of(xh * 160, 16)))
+        for side in range(2)
+    ]
+    for copy in a_copies:
+        copy.start()
+
+    def paired(half, out):
+        @pl.loop(0, 10)
+        def _(ch):
+            row = pl.multiple_of(half * 160 + ch * 16, 16)
+            for side in range(2):
+                own = gv[pl.ds(row, 16), pl.ds(pl.multiple_of(mine + side * 512, 256), 256)]
+                total = own.astype(F32) + ra[pl.ds(row, 16), side * 256 : side * 256 + 256].astype(F32)
+                for eight in range(2):
+                    for tile in range(2):
+                        out[pl.ds(ch * 64 + eight * 32 + side * 2 + tile, 8, stride=4), :] = total[
+                            eight * 8 : eight * 8 + 8, tile * 128 : tile * 128 + 128
+                        ]
+
+    def place(i):
+        return lax.rem(z + far_first(i), 16)
+
+    def rows_of(ref, zz):
+        return ref[pl.ds(pl.multiple_of(zz * 40, 8), 40), :]
+
+    def x_copy(i):
+        return remote(xs.at[place(i)], xr.at[place(i)], xsem_s.at[i], xsem_r.at[place(i)], p, xmate)
+
+    a_copies[0].wait_recv()
+    a_copies[1].wait_recv()
+    paired(1 - xh, xo32)
+
+    @pl.loop(0, 16)
+    def _(i):
+        xs[place(i)] = rows_of(xo32, place(i)).astype(BF16).reshape(5, 8, 128)
+        x_copy(i).start()
+
+    a_copies[2].wait_recv()
+    a_copies[3].wait_recv()
+    paired(xh, z32)
+
+    def z_copy(i):
+        return remote(zs.at[place(i)], rz.at[z], zsem_s.at[i], zsem_r.at[z], p, zdev(place(i)))
+
+    @pl.loop(0, 15)
+    def _(i):
+        x_copy(i).wait_recv()
+        piece = rows_of(z32, place(i)) + xr[place(i)].astype(F32).reshape(40, 128)
+        zs[place(i)] = piece.astype(BF16).reshape(5, 8, 128)
+        z_copy(i).start()
+
+    x_copy(15).wait_recv()
+    sz[0:40, :] = rows_of(z32, z) + xr[z].astype(F32).reshape(40, 128)
+    sz[40:64, :] = jnp.zeros((24, 128), F32)
 
     local[1].wait()
     local[2].wait()
@@ -104,84 +178,18 @@
     for j in range(4):
         for m in range(4):
             qs[j, m * 16 : m * 16 + 16, 0:160] = queries[m * 64 + j * 16 : m * 64 + j * 16 + 16]
-    local[0].wait()
-    pl.semaphore_wait(barrier, 39 - has_self)
-
-    def remote(src, dst, send, recv, section, replica):
-        return pltpu.make_async_remote_copy(
-            src_ref=src, dst_ref=dst, send_sem=send, recv_sem=recv,
-            device_id={"section": section, "replica": replica}, device_id_type=MESH,
-        )
-
-    theirs = pl.multiple_of((1 - core) * 256, 256)
-    mine = pl.multiple_of(core * 256, 256)
-    a_copies = [
-        remote(gv.at[:, pl.ds(pl.multiple_of(theirs + side * 512, 256), 256)],
-               ra.at[:, pl.ds(side * 256, 256)], asem_s.at[side], asem_r.at[side], p, mate)
-        for side in range(2)
-    ]
-    for copy in a_copies:
-        copy.start()
 
     def q_copy(i):
         other = lax.rem(quarter + i, 4)
-        return remote(qs.at[other], qr.at[quarter], qsem_s.at[i], qsem_r.at[quarter], kv_head * 4 + other, r)
+        return remote(
+            qs.at[lax.rem(other + 2, 4)], qr.at[quarter], qsem_s.at[i], qsem_r.at[quarter], kv_head * 4 + other, r
+        )
 
     @pl.loop(1, 4)
     def _(i):
         q_copy(i).start()
 
-    qr[quarter] = qs[quarter]
-    for copy in a_copies:
-        copy.wait_recv()
-
-    def paired(row, side):
-        own = gv[pl.ds(row, 16), pl.ds(pl.multiple_of(mine + side * 512, 256), 256)]
-        return own.astype(F32) + ra[pl.ds(row, 16), pl.ds(side * 256, 256)].astype(F32)
-
-    @pl.loop(0, 10)
-    def _(ch):
-        row = pl.multiple_of((1 - xh) * 160 + ch * 16, 16)
-        for side in range(2):
-            xs[pl.ds(pl.multiple_of(ch * 16, 16), 16), side * 256 : side * 256 + 256] = paired(row, side).astype(BF16)
-
-    b_copy = remote(xs, rb, bsem_s, bsem_r, p, xmate)
-    b_copy.start()
-    b_copy.wait_recv()
-
-    @pl.loop(0, 10)
-    def _(ch):
-        row = pl.multiple_of(xh * 160 + ch * 16, 16)
-        part = pl.multiple_of(ch * 16, 16)
-        for side in range(2):
-            total = paired(row, side) + rb[pl.ds(part, 16), side * 256 : side * 256 + 256].astype(F32)
-            for half in range(2):
-                for tile in range(2):
-                    z32[pl.ds(ch * 64 + half * 32 + side * 2 + tile, 8, stride=4), :] = total[
-                        half * 8 : half * 8 + 8, tile * 128 : tile * 128 + 128
-                    ]
-
-    def z_copy(i):
-        other = lax.rem(z + far_first(i), 16)
-        return remote(zs.at[other], rz.at[z], zsem_s.at[i], zsem_r.at[z], p, zdev(other))
-
-    @pl.loop(0, 15)
-    def _(i):
-        other = lax.rem(z + far_first(i), 16)
-        piece = z32[pl.ds(pl.multiple_of(other * 40, 8), 40), :]
-        zs[other] = piece.astype(BF16).reshape(5, 8, 128)
-        z_copy(i).start()
-
-    @pl.loop(1, 4)
-    def _(i):
-        other = lax.rem(quarter + i, 4)
-        remote(qs.at[other], qr.at[other], qsem_s.at[i], qsem_r.at[other], kv_head * 4 + other, r).wait_recv()
-
-    for j in range(4):
-        qall[:, j * 160 : j * 160 + 160] = qr[j, :, 0:160]
-
-    sz[0:40, :] = z32[pl.ds(pl.multiple_of(z * 40, 8), 40), :]
-    sz[40:64, :] = jnp.zeros((24, 128), F32)
+    qr[quarter] = qs[served]
 
     @pl.loop(0, 15)
     def _(i):
@@ -216,6 +224,14 @@
     def _():
         rs[p] = ss[core * 8 + lax.rem(p, 8)]
 
+    @pl.loop(1, 4)
+    def _(i):
+        other = lax.rem(quarter + i, 4)
+        remote(qs.at[other], qr.at[other], qsem_s.at[i], qsem_r.at[other], kv_head * 4 + other, r).wait_recv()
+
+    for j in range(4):
+        qall[:, j * 160 : j * 160 + 160] = qr[j, :, 0:160]
+
     for copy in local[3:]:
         copy.wait()
 
@@ -264,6 +280,14 @@
     gx_copy(15, r).start()
     gm_copy(31, r).start()
     scatter(r)
+
+    def xslot(i):
+        far = jnp.where(i == 0, 0, near_first(i - 1))
+        return (1 - xh) * 32 + lax.rem(z + far, 16) * 2 + core
+
+    def from_mate(slot):
+        arrive(slot + 1 - 2 * core)
+        scatter(slot + 1 - 2 * core)
 
     @pl.loop(0, 15)
     def _(i):
@@ -272,10 +296,7 @@
         gx_copy(i, slot).start()
         gm_copy(i, slot).start()
         scatter(slot)
-
-    def xslot(i):
-        far = jnp.where(i == 0, 0, near_first(i - 1))
-        return (1 - xh) * 32 + lax.rem(z + far, 16) * 2 + core
+        from_mate(zdev(lax.rem(z + jnp.where(i == 0, 0, near_first(i - 1)), 16)))
 
     @pl.loop(0, 16)
     def _(i):
@@ -283,12 +304,9 @@
         arrive(slot)
         gm_copy(15 + i, slot).start()
         scatter(slot)
-
-    @pl.loop(0, 32)
-    def _(i):
-        slot = i * 2 + 1 - core
-        arrive(slot)
-        scatter(slot)
+        from_mate(jnp.where(i == 0, zdev(lax.rem(z + 8, 16)), xslot(i - 1)))
+
+    from_mate(xslot(15))
 
     w2b[...] = w2[...].astype(BF16)
     low = jnp.dot(hv[:, :2560], w2b[...], preferred_element_type=F32)
@@ -327,7 +345,7 @@
         dest[(turn // 2) * 128 : (turn // 2) * 128 + 128, :] = merged.astype(BF16)
 
     token = lax.broadcasted_iota(jnp.int32, (64, 256), 0)
-    position = lax.div(token, 16) * 64 + lax.rem(token, 16) + quarter * 16
+    position = lax.div(token, 16) * 64 + lax.rem(token, 16) + served * 16
     key_pos = lax.broadcasted_iota(jnp.int32, (64, 256), 1)
     length = len_ref[0]
     allowed = jnp.logical_and(key_pos <= position, key_pos < length)
@@ -345,32 +363,31 @@
             cs[m, :, h * 128 : h * 128 + 128] = mixed[m * 16 : m * 16 + 16]
 
     def c_copy(i):
-        other = lax.rem(kv_head + i, 4)
-        return remote(cs.at[other], cr.at[kv_head], csem_s.at[i], csem_r.at[kv_head], other * 4 + quarter, r)
-
-    @pl.loop(1, 4)
+        other = lax.rem(kv_head + 2 + i, 4)
+        return remote(cs.at[other], cr.at[kv_head], csem_s.at[i], csem_r.at[kv_head], other * 4 + served, r)
+
+    @pl.loop(0, 4)
     def _(i):
         c_copy(i).start()
 
-    cr[kv_head] = cs[kv_head]
-
-    @pl.loop(1, 4)
-    def _(i):
-        other = lax.rem(kv_head + i, 4)
-        remote(cs.at[other], cr.at[other], csem_s.at[i], csem_r.at[other], other * 4 + quarter, r).wait_recv()
+    @pl.loop(0, 4)
+    def _(i):
+        remote(cs.at[i], cr.at[i], csem_s.at[i], csem_r.at[i], i * 4 + served, r).wait_recv()
 
     for m in range(4):
         ctx_ref[:, m * 640 : m * 640 + 640] = cr[m].astype(F32)
 
     for copy in a_copies:
         copy.wait_send()
-    b_copy.wait_send()
+
+    @pl.loop(0, 4)
+    def _(i):
+        c_copy(i).wait_send()
 
     @pl.loop(1, 4)
     def _(i):
         q_copy(i).wait_send()
         k_copy(i).wait_send()
-        c_copy(i).wait_send()
 
     @pl.loop(0, 15)
     def _(i):
@@ -385,6 +402,7 @@
     @pl.loop(0, 16)
     def _(i):
         gm_copy(15 + i, xslot(i)).wait_send()
+        x_copy(i).wait_send()
 
         @pl.when(jnp.logical_not(s_here(i)))
         def _():
@@ -411,8 +429,9 @@
             vm((160, 5120), BF16),
             vm((80, 1, 64), F32), vm((80, 1, 64), F32), vm((80, 1, 64), F32),
             vm((320, 512), BF16),
-            vm((160, 512), BF16),
-            vm((160, 512), BF16),
+            vm((640, 128), F32),
+            vm((16, 5, 8, 128), BF16),
+            vm((16, 5, 8, 128), BF16),
             vm((640, 128), F32),
             vm((16, 5, 8, 128), BF16),
             vm((16, 5, 8, 128), BF16),
@@ -432,7 +451,7 @@
             vm((256, 128), BF16),
             vm((4, 16, 640), BF16),
             vm((4, 16, 640), BF16),
-            dma((6,)), dma((2,)), dma((2,)), dma, dma, dma((15,)), dma((16,)),
+            dma((6,)), dma((4,)), dma((4,)), dma((16,)), dma((16,)), dma((15,)), dma((16,)),
             dma((16,)), dma((16,)), dma((15,)), dma((16,)), dma((32,)), dma((64,)),
             dma((4,)), dma((4,)), dma((4,)), dma((4,)), dma((4,)), dma((4,)),
         ],
@@ -441,9 +460,32 @@
     )(gradients, tokens, query_weight_t, master, first, second, lengths)
 
 
+def finish_kernel(*refs):
+    sources, targets, held, came, left = refs[:4], refs[4:8], refs[8:12], refs[12], refs[13]
+    for i in range(4):
+        pltpu.make_async_copy(sources[i], held[i], came.at[i]).start()
+    for i in range(4):
+        pltpu.make_async_copy(sources[i], held[i], came.at[i]).wait()
+        pltpu.make_async_copy(held[i], targets[i], left.at[i]).start()
+    for i in range(4):
+        pltpu.make_async_copy(held[i], targets[i], left.at[i]).wait()
+
+
+def finish(arrays):
+    anyspace = pl.BlockSpec(memory_space=pl.ANY)
+    return pl.pallas_call(
+        finish_kernel,
+        out_shape=[jax.ShapeDtypeStruct(a.shape, a.dtype) for a in arrays],
+        in_specs=[anyspace] * 4,
+        out_specs=[anyspace] * 4,
+        scratch_shapes=[pltpu.VMEM(a.shape, a.dtype) for a in arrays] + [pltpu.SemaphoreType.DMA((4,))] * 2,
+        name="finish",
+    )(*arrays)
+
+
 def on_device(gradients, hidden, lengths, query_weight, master, first_moment, second_moment):
     states = [a.reshape(80, 1, 64) for a in (master, first_moment, second_moment)]
-    *states, context = update(gradients[0], hidden[0], query_weight.T, *states, lengths)
+    *states, context = finish(update(gradients[0], hidden[0], query_weight.T, *states, lengths))
     return (*[a.reshape(16, 1, 5, 64) for a in states], context[None])
 
 

time: 85.5 us -> 84.8 us (level)
  local copies, waits for them, and re-layouts: 5.81 us -> 0 us
  Pallas kernels: 77.6 us -> 82.5 us
    unnamed x4 -> x0, local copies, waits for them, and re-layouts: 5.81 us -> none
    pallas_call x1, Pallas kernels: 77.6 us -> 80.8 us  [update(): pl.pallas_call(update_kernel, out_shape=(state, state, state, jax.ShapeDt...]
    pallas_call x0 -> x1, Pallas kernels: none -> 1.73 us  [finish(): pl.pallas_call(finish_kernel, out_shape=[jax.ShapeDtypeStruct(a.shape, a....]
where the time goes in v3:
time: 84.8 us; the launch traced here: 83.8 us
  Pallas kernels  82.5 us (97%)
  between operations  1.29 us (2%)
    pallas_call x1, Pallas kernels, update(): pl.pallas_call(update_kernel, out_shape=(state, state, state, jax.ShapeDt...  80.8 us
    pallas_call x1, Pallas kernels, finish(): pl.pallas_call(finish_kernel, out_shape=[jax.ShapeDtypeStruct(a.shape, a....  1.73 us

profile of v3, /device:TPU:1, one launch (start us, length us, event | category | flops | bytes accessed | tf_op | source)
XLA Modules:
  0.0 83.8 jit_solution(15039437263455840905)
XLA Ops:
  1.3 80.8 %update.1 = (f32[80,1,64]{2,1,0:T(1,128)}, f32[80,1,64]{2,1,0:T(1,128)}, f32[80,1,64]{2,1,0:T(1,128)}, f32[16,2560]{1,0:T(8,128)}) custom-call(bf16[320,1024]{1,0:T(8,128)(2,1)} %bitcast.12, bf16[256,5120]{1,0:T(8,128)(2,1)} %bitcast.10, bf16[160,5120]{1,0:T(8,128)(2,1)} %bitcast.11, f32[80,1,64]{2,1,0:T(1,128)} %bitcast.13, f32[80,1,64]{2,1,0:T(1,128)} %bitcast.14, ...), custom_call_target="tpu_custom_call" | custom-call | tf_op jit(solution)/shard_map/update/pallas_call | solution.py:418
  82.1 1.7 %finish.1 = (f32[80,1,64]{2,1,0:T(1,128)}, f32[80,1,64]{2,1,0:T(1,128)}, f32[80,1,64]{2,1,0:T(1,128)}, f32[16,2560]{1,0:T(8,128)}) custom-call(f32[80,1,64]{2,1,0:T(1,128)} %get-tuple-element.12.refs_0_, f32[80,1,64]{2,1,0:T(1,128)} %get-tuple-element.13.refs_1_, f32[80,1,64]{2,1,0:T(1,128)} %get-tuple-element.14.refs_2_, f32[16,2560]{1,0:T(8,128)} %get-tuple-element.15.refs_3_), custom_call_target="tpu_custom_call" | custom-call | tf_op jit(solution)/shard_map/finish/pallas_call | solution.py:476

commit v4 on v3

--- a/solution.py
+++ b/solution.py
@@ -258,7 +258,7 @@
         agb[r, k] = m2[pl.ds(k, 8, stride=8), :].astype(BF16)
 
     def gz_copy(i):
-        return remote(agb.at[r], agb.at[r], gz_s.at[i], g_r.at[r], p, zdev(lax.rem(z + far_first(i), 16)))
+        return remote(agb.at[r], agb.at[r], gz_s.at[i], g_r.at[r], p, zdev(lax.rem(z + near_first(i), 16)))
 
     def gx_copy(i, slot):
         return remote(agb.at[slot], agb.at[slot], gx_s.at[i], g_r.at[slot], p, xmate)
@@ -273,11 +273,12 @@
         for k in range(5):
             w2[pl.ds(slot * 5 + k, 8, stride=320), :] = agb[slot, k].astype(F32)
 
+    gx_copy(15, r).start()
+
     @pl.loop(0, 15)
     def _(i):
         gz_copy(i).start()
 
-    gx_copy(15, r).start()
     gm_copy(31, r).start()
     scatter(r)
 
@@ -296,7 +297,6 @@
         gx_copy(i, slot).start()
         gm_copy(i, slot).start()
         scatter(slot)
-        from_mate(zdev(lax.rem(z + jnp.where(i == 0, 0, near_first(i - 1)), 16)))
 
     @pl.loop(0, 16)
     def _(i):
@@ -304,9 +304,11 @@
         arrive(slot)
         gm_copy(15 + i, slot).start()
         scatter(slot)
-        from_mate(jnp.where(i == 0, zdev(lax.rem(z + 8, 16)), xslot(i - 1)))
-
-    from_mate(xslot(15))
+        from_mate(zdev(lax.rem(z + jnp.where(i == 0, 0, near_first(i - 1)), 16)))
+
+    @pl.loop(0, 16)
+    def _(i):
+        from_mate(xslot(i))
 
     w2b[...] = w2[...].astype(BF16)
     low = jnp.dot(hv[:, :2560], w2b[...], preferred_element_type=F32)

time: 84.8 us -> 80 us (0.943)
  Pallas kernels: 82.5 us -> 78.2 us
    pallas_call x1, Pallas kernels: 80.8 us -> 76.5 us  [update(): pl.pallas_call(update_kernel, out_shape=(state, state, state, jax.ShapeDt...]
where the time goes in v4:
time: 80 us; the launch traced here: 79.5 us
  Pallas kernels  78.2 us (98%)
  between operations  1.29 us (2%)
    pallas_call x1, Pallas kernels, update(): pl.pallas_call(update_kernel, out_shape=(state, state, state, jax.ShapeDt...  76.5 us
    pallas_call x1, Pallas kernels, finish(): pl.pallas_call(finish_kernel, out_shape=[jax.ShapeDtypeStruct(a.shape, a....  1.73 us

profile of v4, /device:TPU:1, one launch (start us, length us, event | category | flops | bytes accessed | tf_op | source)
XLA Modules:
  0.0 79.5 jit_solution(9468361330595747940)
XLA Ops:
  1.3 76.5 %update.1 = (f32[80,1,64]{2,1,0:T(1,128)}, f32[80,1,64]{2,1,0:T(1,128)}, f32[80,1,64]{2,1,0:T(1,128)}, f32[16,2560]{1,0:T(8,128)}) custom-call(bf16[320,1024]{1,0:T(8,128)(2,1)} %bitcast.12, bf16[256,5120]{1,0:T(8,128)(2,1)} %bitcast.10, bf16[160,5120]{1,0:T(8,128)(2,1)} %bitcast.11, f32[80,1,64]{2,1,0:T(1,128)} %bitcast.13, f32[80,1,64]{2,1,0:T(1,128)} %bitcast.14, ...), custom_call_target="tpu_custom_call" | custom-call | tf_op jit(solution)/shard_map/update/pallas_call | solution.py:420
  77.8 1.7 %finish.1 = (f32[80,1,64]{2,1,0:T(1,128)}, f32[80,1,64]{2,1,0:T(1,128)}, f32[80,1,64]{2,1,0:T(1,128)}, f32[16,2560]{1,0:T(8,128)}) custom-call(f32[80,1,64]{2,1,0:T(1,128)} %get-tuple-element.12.refs_0_, f32[80,1,64]{2,1,0:T(1,128)} %get-tuple-element.13.refs_1_, f32[80,1,64]{2,1,0:T(1,128)} %get-tuple-element.14.refs_2_, f32[16,2560]{1,0:T(8,128)} %get-tuple-element.15.refs_3_), custom_call_target="tpu_custom_call" | custom-call | tf_op jit(solution)/shard_map/finish/pallas_call | solution.py:478

commit v5 on v4

--- a/solution.py
+++ b/solution.py
@@ -45,7 +45,7 @@
     nm_ref, nf_ref, ns_ref, ctx_ref,
     gv, hv, qv, ma, fm, sm, ra, xo32, xs, xr, z32, zs, rz, sz, ss, rs, m2, agb, w2, w2b,
     qs, qr, qall, kvs, kvr, keys_all, values_all, cs, cr,
-    lsem, asem_s, asem_r, xsem_s, xsem_r, zsem_s, zsem_r, ssem_s, ssem_r, gz_s, gx_s, gm_s, g_r,
+    lsem, asem_s, asem_r, xsem_s, xsem_r, zsem_s, zsem_r, ssem_s, ssem_r, gz_s, gr_s, gx_s, gm_s, g_r,
     qsem_s, qsem_r, ksem_s, ksem_r, csem_s, csem_r,
 ):
     p = lax.axis_index("section")
@@ -257,8 +257,17 @@
     for k in range(5):
         agb[r, k] = m2[pl.ds(k, 8, stride=8), :].astype(BF16)
 
+    def came(i):
+        index = jnp.where(i < 4, i, jnp.where(i < 6, i + 4, jnp.where(i < 10, i - 2, i)))
+        return lax.rem(z + near_first(index), 16)
+
     def gz_copy(i):
-        return remote(agb.at[r], agb.at[r], gz_s.at[i], g_r.at[r], p, zdev(lax.rem(z + near_first(i), 16)))
+        away = (5, 11, 8, 1, 15, 2, 14)[i]
+        return remote(agb.at[r], agb.at[r], gz_s.at[i], g_r.at[r], p, zdev(lax.rem(z + away, 16)))
+
+    def gr_copy(i, turn, slot):
+        to = zdev(lax.rem(z + (1, 15, 2, 14)[turn], 16))
+        return remote(agb.at[slot], agb.at[slot], gr_s.at[(i - 4) * 4 + turn], g_r.at[slot], p, to)
 
     def gx_copy(i, slot):
         return remote(agb.at[slot], agb.at[slot], gx_s.at[i], g_r.at[slot], p, xmate)
@@ -275,16 +284,13 @@
 
     gx_copy(15, r).start()
 
-    @pl.loop(0, 15)
-    def _(i):
+    for i in range(7):
         gz_copy(i).start()
-
     gm_copy(31, r).start()
     scatter(r)
 
     def xslot(i):
-        far = jnp.where(i == 0, 0, near_first(i - 1))
-        return (1 - xh) * 32 + lax.rem(z + far, 16) * 2 + core
+        return (1 - xh) * 32 + jnp.where(i == 0, z, came(i - 1)) * 2 + core
 
     def from_mate(slot):
         arrive(slot + 1 - 2 * core)
@@ -292,8 +298,14 @@
 
     @pl.loop(0, 15)
     def _(i):
-        slot = zdev(lax.rem(z + near_first(i), 16))
+        slot = zdev(came(i))
         arrive(slot)
+
+        @pl.when(jnp.logical_and(i >= 4, i < 6))
+        def _():
+            for turn in range(4):
+                gr_copy(i, turn, slot).start()
+
         gx_copy(i, slot).start()
         gm_copy(i, slot).start()
         scatter(slot)
@@ -304,7 +316,7 @@
         arrive(slot)
         gm_copy(15 + i, slot).start()
         scatter(slot)
-        from_mate(zdev(lax.rem(z + jnp.where(i == 0, 0, near_first(i - 1)), 16)))
+        from_mate(zdev(jnp.where(i == 0, z, came(i - 1))))
 
     @pl.loop(0, 16)
     def _(i):
@@ -394,10 +406,14 @@
     @pl.loop(0, 15)
     def _(i):
         z_copy(i).wait_send()
+        gx_copy(i, zdev(came(i))).wait_send()
+        gm_copy(i, zdev(came(i))).wait_send()
+
+    for i in range(7):
         gz_copy(i).wait_send()
-        gx_copy(i, zdev(lax.rem(z + near_first(i), 16))).wait_send()
-        gm_copy(i, zdev(lax.rem(z + near_first(i), 16))).wait_send()
-
+    for i in (4, 5):
+        for turn in range(4):
+            gr_copy(i, turn, zdev(came(i))).wait_send()
     gx_copy(15, r).wait_send()
     gm_copy(31, r).wait_send()
 
@@ -454,7 +470,7 @@
             vm((4, 16, 640), BF16),
             vm((4, 16, 640), BF16),
             dma((6,)), dma((4,)), dma((4,)), dma((16,)), dma((16,)), dma((15,)), dma((16,)),
-            dma((16,)), dma((16,)), dma((15,)), dma((16,)), dma((32,)), dma((64,)),
+            dma((16,)), dma((16,)), dma((7,)), dma((8,)), dma((16,)), dma((32,)), dma((64,)),
             dma((4,)), dma((4,)), dma((4,)), dma((4,)), dma((4,)), dma((4,)),
         ],
         compiler_params=pltpu.CompilerParams(collective_id=0, has_side_effects=True),

time: 80 us -> 77.7 us (0.971)
  Pallas kernels: 78.2 us -> 75.9 us
    pallas_call x1, Pallas kernels: 76.5 us -> 74.2 us  [update(): pl.pallas_call(update_kernel, out_shape=(state, state, state, jax.ShapeDt...]
where the time goes in v5:
time: 77.7 us; the launch traced here: 77.2 us
  Pallas kernels  75.9 us (98%)
  between operations  1.29 us (2%)
    pallas_call x1, Pallas kernels, update(): pl.pallas_call(update_kernel, out_shape=(state, state, state, jax.ShapeDt...  74.2 us
    pallas_call x1, Pallas kernels, finish(): pl.pallas_call(finish_kernel, out_shape=[jax.ShapeDtypeStruct(a.shape, a....  1.73 us

profile of v5, /device:TPU:1, one launch (start us, length us, event | category | flops | bytes accessed | tf_op | source)
XLA Modules:
  0.0 77.2 jit_solution(1504585526042539486)
XLA Ops:
  1.3 74.2 %update.1 = (f32[80,1,64]{2,1,0:T(1,128)}, f32[80,1,64]{2,1,0:T(1,128)}, f32[80,1,64]{2,1,0:T(1,128)}, f32[16,2560]{1,0:T(8,128)}) custom-call(bf16[320,1024]{1,0:T(8,128)(2,1)} %bitcast.12, bf16[256,5120]{1,0:T(8,128)(2,1)} %bitcast.10, bf16[160,5120]{1,0:T(8,128)(2,1)} %bitcast.11, f32[80,1,64]{2,1,0:T(1,128)} %bitcast.13, f32[80,1,64]{2,1,0:T(1,128)} %bitcast.14, ...), custom_call_target="tpu_custom_call" | custom-call | tf_op jit(solution)/shard_map/update/pallas_call | solution.py:436
  75.5 1.7 %finish.1 = (f32[80,1,64]{2,1,0:T(1,128)}, f32[80,1,64]{2,1,0:T(1,128)}, f32[80,1,64]{2,1,0:T(1,128)}, f32[16,2560]{1,0:T(8,128)}) custom-call(f32[80,1,64]{2,1,0:T(1,128)} %get-tuple-element.12.refs_0_, f32[80,1,64]{2,1,0:T(1,128)} %get-tuple-element.13.refs_1_, f32[80,1,64]{2,1,0:T(1,128)} %get-tuple-element.14.refs_2_, f32[16,2560]{1,0:T(8,128)} %get-tuple-element.15.refs_3_), custom_call_target="tpu_custom_call" | custom-call | tf_op jit(solution)/shard_map/finish/pallas_call | solution.py:494

commit v6 on v5

--- a/solution.py
+++ b/solution.py
@@ -258,16 +258,17 @@
         agb[r, k] = m2[pl.ds(k, 8, stride=8), :].astype(BF16)
 
     def came(i):
-        index = jnp.where(i < 4, i, jnp.where(i < 6, i + 4, jnp.where(i < 10, i - 2, i)))
+        late = jnp.where(i == 6, 14, jnp.where(i < 11, i - 3, i - 1))
+        index = jnp.where(i < 4, i, jnp.where(i < 6, i + 4, late))
         return lax.rem(z + near_first(index), 16)
 
     def gz_copy(i):
         away = (5, 11, 8, 1, 15, 2, 14)[i]
         return remote(agb.at[r], agb.at[r], gz_s.at[i], g_r.at[r], p, zdev(lax.rem(z + away, 16)))
 
-    def gr_copy(i, turn, slot):
+    def gr_copy(at, turn, slot):
         to = zdev(lax.rem(z + (1, 15, 2, 14)[turn], 16))
-        return remote(agb.at[slot], agb.at[slot], gr_s.at[(i - 4) * 4 + turn], g_r.at[slot], p, to)
+        return remote(agb.at[slot], agb.at[slot], gr_s.at[at * 4 + turn], g_r.at[slot], p, to)
 
     def gx_copy(i, slot):
         return remote(agb.at[slot], agb.at[slot], gx_s.at[i], g_r.at[slot], p, xmate)
@@ -296,7 +297,10 @@
         arrive(slot + 1 - 2 * core)
         scatter(slot + 1 - 2 * core)
 
-    @pl.loop(0, 15)
+    def own_ring(i):
+        return zdev(jnp.where(i == 0, z, came(i - 1)))
+
+    @pl.loop(0, 7)
     def _(i):
         slot = zdev(came(i))
         arrive(slot)
@@ -304,21 +308,43 @@
         @pl.when(jnp.logical_and(i >= 4, i < 6))
         def _():
             for turn in range(4):
-                gr_copy(i, turn, slot).start()
+                gr_copy(i - 4, turn, slot).start()
 
         gx_copy(i, slot).start()
         gm_copy(i, slot).start()
         scatter(slot)
 
-    @pl.loop(0, 16)
+    @pl.loop(0, 8)
+    def _(i):
+        slot = xslot(i)
+        arrive(slot)
+
+        @pl.when(jnp.logical_and(i >= 5, i < 7))
+        def _():
+            for turn in range(4):
+                gr_copy(i - 3, turn, slot).start()
+
+        gm_copy(15 + i, slot).start()
+        scatter(slot)
+        from_mate(own_ring(i))
+
+    @pl.loop(7, 15)
+    def _(i):
+        slot = zdev(came(i))
+        arrive(slot)
+        gm_copy(i, slot).start()
+        scatter(slot)
+        from_mate(xslot(i - 7))
+
+    @pl.loop(8, 16)
     def _(i):
         slot = xslot(i)
         arrive(slot)
         gm_copy(15 + i, slot).start()
         scatter(slot)
-        from_mate(zdev(jnp.where(i == 0, z, came(i - 1))))
-
-    @pl.loop(0, 16)
+        from_mate(own_ring(i))
+
+    @pl.loop(8, 16)
     def _(i):
         from_mate(xslot(i))
 
@@ -406,14 +432,15 @@
     @pl.loop(0, 15)
     def _(i):
         z_copy(i).wait_send()
-        gx_copy(i, zdev(came(i))).wait_send()
         gm_copy(i, zdev(came(i))).wait_send()
 
     for i in range(7):
         gz_copy(i).wait_send()
-    for i in (4, 5):
+        gx_copy(i, zdev(came(i))).wait_send()
+    for at in range(2):
         for turn in range(4):
-            gr_copy(i, turn, zdev(came(i))).wait_send()
+            gr_copy(at, turn, zdev(came(at + 4))).wait_send()
+            gr_copy(at + 2, turn, xslot(at + 5)).wait_send()
     gx_copy(15, r).wait_send()
     gm_copy(31, r).wait_send()
 
@@ -470,7 +497,7 @@
             vm((4, 16, 640), BF16),
             vm((4, 16, 640), BF16),
             dma((6,)), dma((4,)), dma((4,)), dma((16,)), dma((16,)), dma((15,)), dma((16,)),
-            dma((16,)), dma((16,)), dma((7,)), dma((8,)), dma((16,)), dma((32,)), dma((64,)),
+            dma((16,)), dma((16,)), dma((7,)), dma((16,)), dma((16,)), dma((32,)), dma((64,)),
             dma((4,)), dma((4,)), dma((4,)), dma((4,)), dma((4,)), dma((4,)),
         ],
         compiler_params=pltpu.CompilerParams(collective_id=0, has_side_effects=True),

time: 77.7 us -> 76.9 us (0.990)
  no operation moved by 1% of the time
where the time goes in v6:
time: 76.9 us; the launch traced here: 76.8 us
  Pallas kernels  75.5 us (98%)
  between operations  1.29 us (2%)
    pallas_call x1, Pallas kernels, update(): pl.pallas_call(update_kernel, out_shape=(state, state, state, jax.ShapeDt...  73.7 us
    pallas_call x1, Pallas kernels, finish(): pl.pallas_call(finish_kernel, out_shape=[jax.ShapeDtypeStruct(a.shape, a....  1.73 us

profile of v6, /device:TPU:1, one launch (start us, length us, event | category | flops | bytes accessed | tf_op | source)
XLA Modules:
  0.0 76.8 jit_solution(1556319586874701479)
XLA Ops:
  1.3 73.7 %update.1 = (f32[80,1,64]{2,1,0:T(1,128)}, f32[80,1,64]{2,1,0:T(1,128)}, f32[80,1,64]{2,1,0:T(1,128)}, f32[16,2560]{1,0:T(8,128)}) custom-call(bf16[320,1024]{1,0:T(8,128)(2,1)} %bitcast.12, bf16[256,5120]{1,0:T(8,128)(2,1)} %bitcast.10, bf16[160,5120]{1,0:T(8,128)(2,1)} %bitcast.11, f32[80,1,64]{2,1,0:T(1,128)} %bitcast.13, f32[80,1,64]{2,1,0:T(1,128)} %bitcast.14, ...), custom_call_target="tpu_custom_call" | custom-call | tf_op jit(solution)/shard_map/update/pallas_call | solution.py:463
  75.0 1.7 %finish.1 = (f32[80,1,64]{2,1,0:T(1,128)}, f32[80,1,64]{2,1,0:T(1,128)}, f32[80,1,64]{2,1,0:T(1,128)}, f32[16,2560]{1,0:T(8,128)}) custom-call(f32[80,1,64]{2,1,0:T(1,128)} %get-tuple-element.12.refs_0_, f32[80,1,64]{2,1,0:T(1,128)} %get-tuple-element.13.refs_1_, f32[80,1,64]{2,1,0:T(1,128)} %get-tuple-element.14.refs_2_, f32[16,2560]{1,0:T(8,128)} %get-tuple-element.15.refs_3_), custom_call_target="tpu_custom_call" | custom-call | tf_op jit(solution)/shard_map/finish/pallas_call | solution.py:521

commit v7 on v6

--- a/solution.py
+++ b/solution.py
@@ -171,26 +171,6 @@
     sz[0:40, :] = rows_of(z32, z) + xr[z].astype(F32).reshape(40, 128)
     sz[40:64, :] = jnp.zeros((24, 128), F32)
 
-    local[1].wait()
-    local[2].wait()
-    queries = lax.dot_general(hv[...], qv[...], (((1,), (1,)), ((), ())), preferred_element_type=F32)
-    queries = queries.astype(BF16)
-    for j in range(4):
-        for m in range(4):
-            qs[j, m * 16 : m * 16 + 16, 0:160] = queries[m * 64 + j * 16 : m * 64 + j * 16 + 16]
-
-    def q_copy(i):
-        other = lax.rem(quarter + i, 4)
-        return remote(
-            qs.at[lax.rem(other + 2, 4)], qr.at[quarter], qsem_s.at[i], qsem_r.at[quarter], kv_head * 4 + other, r
-        )
-
-    @pl.loop(1, 4)
-    def _(i):
-        q_copy(i).start()
-
-    qr[quarter] = qs[served]
-
     @pl.loop(0, 15)
     def _(i):
         other = lax.rem(z + near_first(i), 16)
@@ -224,13 +204,25 @@
     def _():
         rs[p] = ss[core * 8 + lax.rem(p, 8)]
 
+    local[1].wait()
+    local[2].wait()
+    queries = lax.dot_general(hv[...], qv[...], (((1,), (1,)), ((), ())), preferred_element_type=F32)
+    queries = queries.astype(BF16)
+    for j in range(4):
+        for m in range(4):
+            qs[j, m * 16 : m * 16 + 16, 0:160] = queries[m * 64 + j * 16 : m * 64 + j * 16 + 16]
+
+    def q_copy(i):
+        other = lax.rem(quarter + i, 4)
+        return remote(
+            qs.at[lax.rem(other + 2, 4)], qr.at[quarter], qsem_s.at[i], qsem_r.at[quarter], kv_head * 4 + other, r
+        )
+
     @pl.loop(1, 4)
     def _(i):
-        other = lax.rem(quarter + i, 4)
-        remote(qs.at[other], qr.at[other], qsem_s.at[i], qsem_r.at[other], kv_head * 4 + other, r).wait_recv()
-
-    for j in range(4):
-        qall[:, j * 160 : j * 160 + 160] = qr[j, :, 0:160]
+        q_copy(i).start()
+
+    qr[quarter] = qs[served]
 
     for copy in local[3:]:
         copy.wait()
@@ -290,6 +282,14 @@
     gm_copy(31, r).start()
     scatter(r)
 
+    @pl.loop(1, 4)
+    def _(i):
+        other = lax.rem(quarter + i, 4)
+        remote(qs.at[other], qr.at[other], qsem_s.at[i], qsem_r.at[other], kv_head * 4 + other, r).wait_recv()
+
+    for j in range(4):
+        qall[:, j * 160 : j * 160 + 160] = qr[j, :, 0:160]
+
     def xslot(i):
         return (1 - xh) * 32 + jnp.where(i == 0, z, came(i - 1)) * 2 + core
 
@@ -358,13 +358,15 @@
     kvs[...] = pltpu.roll(both, quarter * 32, 1).astype(BF16)
 
     def k_copy(i):
-        return remote(
-            kvs, kvr.at[quarter], ksem_s.at[i], ksem_r.at[quarter], kv_head * 4 + lax.rem(quarter + i, 4), r
-        )
-
-    @pl.loop(1, 4)
-    def _(i):
-        k_copy(i).start()
+        return remote(kvs, kvr.at[quarter], ksem_s.at[i], ksem_r.at[quarter], kv_head * 4 + i, r)
+
+    @pl.loop(0, 4)
+    def _(i):
+        far_end = jnp.where(quarter < 2, 3 - i, i)
+
+        @pl.when(far_end != quarter)
+        def _():
+            k_copy(far_end).start()
 
     kvr[quarter] = kvs[...]
 
@@ -427,7 +429,7 @@
     @pl.loop(1, 4)
     def _(i):
         q_copy(i).wait_send()
-        k_copy(i).wait_send()
+        k_copy(lax.rem(quarter + i, 4)).wait_send()
 
     @pl.loop(0, 15)
     def _(i):

time: 76.9 us -> 77.7 us (1.010)
  Pallas kernels: 75.5 us -> 76.3 us
    pallas_call x1, Pallas kernels: 73.7 us -> 74.5 us  [update(): pl.pallas_call(update_kernel, out_shape=(state, state, state, jax.ShapeDt...]
where the time goes in v7:
time: 77.7 us; the launch traced here: 77.6 us
  Pallas kernels  76.3 us (98%)
  between operations  1.29 us (2%)
    pallas_call x1, Pallas kernels, update(): pl.pallas_call(update_kernel, out_shape=(state, state, state, jax.ShapeDt...  74.5 us
    pallas_call x1, Pallas kernels, finish(): pl.pallas_call(finish_kernel, out_shape=[jax.ShapeDtypeStruct(a.shape, a....  1.73 us

profile of v7, /device:TPU:1, one launch (start us, length us, event | category | flops | bytes accessed | tf_op | source)
XLA Modules:
  0.0 77.6 jit_solution(14774481827552572090)
XLA Ops:
  1.3 74.5 %update.1 = (f32[80,1,64]{2,1,0:T(1,128)}, f32[80,1,64]{2,1,0:T(1,128)}, f32[80,1,64]{2,1,0:T(1,128)}, f32[16,2560]{1,0:T(8,128)}) custom-call(bf16[320,1024]{1,0:T(8,128)(2,1)} %bitcast.12, bf16[256,5120]{1,0:T(8,128)(2,1)} %bitcast.10, bf16[160,5120]{1,0:T(8,128)(2,1)} %bitcast.11, f32[80,1,64]{2,1,0:T(1,128)} %bitcast.13, f32[80,1,64]{2,1,0:T(1,128)} %bitcast.14, ...), custom_call_target="tpu_custom_call" | custom-call | tf_op jit(solution)/shard_map/update/pallas_call | solution.py:465
  75.8 1.7 %finish.1 = (f32[80,1,64]{2,1,0:T(1,128)}, f32[80,1,64]{2,1,0:T(1,128)}, f32[80,1,64]{2,1,0:T(1,128)}, f32[16,2560]{1,0:T(8,128)}) custom-call(f32[80,1,64]{2,1,0:T(1,128)} %get-tuple-element.12.refs_0_, f32[80,1,64]{2,1,0:T(1,128)} %get-tuple-element.13.refs_1_, f32[80,1,64]{2,1,0:T(1,128)} %get-tuple-element.14.refs_2_, f32[16,2560]{1,0:T(8,128)} %get-tuple-element.15.refs_3_), custom_call_target="tpu_custom_call" | custom-call | tf_op jit(solution)/shard_map/finish/pallas_call | solution.py:523
